TPU v7x, 128 devices: a whole 4x4x4 slice. The times are simulated.
128 devices in a mesh: dp: 64 (over y, z_lo, x, core), rep: 2 (over z_hi).
Axes of the slice: x: 4, y: 4, z: 4 (z_hi: 2, z_lo: 2; z = z_hi * 2 + z_lo), core: 2. Of those that a mesh axis runs over, the one named last changes fastest.
Arguments:
- queries: bfloat16 [8192, 2048], P(('dp', 'rep')), may hold values from -24 to 24
- documents: bfloat16 [8192, 2048], P(('dp', 'rep')), may hold values from -24 to 24
- partner: int32 [8192], P(('dp', 'rep')), may hold values from 0 to 8191, each once
Outputs:
- grad_queries: float32 [8192, 2048], P(('dp', 'rep'))
- grad_documents: float32 [8192, 2048], P(('dp', 'rep'))
Inputs may be any that keep to these rules, and one draw needn't show every extreme that they name: `partner`: every document index appears exactly once.
All inputs are finite; a program needn't handle non-finite values.
Results may differ from a plain program's by a relative error of at most 0.0031.
Values may be sent and summed in bfloat16 or wider, within the bound.
A program may use at most 256 MiB of HBM per device.

v0:
```python
import jax
import jax.numpy as jnp
from jax import lax
from jax.sharding import Mesh
from jax.sharding import PartitionSpec as P

WIDTHS = 9
DP = ("dp_0", "dp_1", "dp_2", "dp_3")
DP_REP = ("dp_0", "dp_1", "dp_2", "dp_3", "rep")


logit_gain = 3.0


def laid_out(blocks, dim):
    blocks = jnp.moveaxis(blocks, 0, dim)
    shape = blocks.shape
    return blocks.reshape(*shape[:dim], shape[dim] * shape[dim + 1], *shape[dim + 2 :])


def copy_for_each(x, axis):
    copies = jnp.broadcast_to(x, (lax.axis_size(axis), *x.shape))
    return lax.all_to_all(copies, axis, split_axis=0, concat_axis=0, tiled=True)


def collect(x, axis, dim):
    return laid_out(copy_for_each(x, axis), dim)


def collected_together(x, axis):
    leaves = jax.tree.leaves(x)
    turns = sorted(range(len(leaves)), key=lambda k: -leaves[k].size)
    width = (1, *leaves[turns[0]].shape)[-1]
    lines = [
        jnp.pad(leaves[k].reshape(-1), (0, -leaves[k].size % width)).reshape(-1, width)
        for k in turns
    ]
    both, at, found = (copy_for_each(jnp.concatenate(lines), axis), 0, {})
    for k, line in zip(turns, lines):
        piece = both[:, at : at + len(line)].reshape(len(both), -1)
        found[k] = piece[:, : leaves[k].size].reshape(-1, *leaves[k].shape)
        at += len(line)
    numbers = iter(range(len(leaves)))
    return jax.tree.map(lambda _: found[next(numbers)], x)


def folded_in_pairs(pieces, combine):
    while len(jax.tree.leaves(pieces)[0]) > 1:
        pieces = jax.vmap(combine)(
            *(jax.tree.map(lambda part: part[side::2], pieces) for side in (0, 1))
        )
    return jax.tree.map(lambda part: part[0], pieces)


def merged(x, axis, combine):
    pieces = collected_together(x, axis)
    return folded_in_pairs(pieces, combine)


def cut_along(x, dim, size):
    shape = x.shape
    blocks = x.reshape(*shape[:dim], size, shape[dim] // size, *shape[dim + 1 :])
    return jnp.moveaxis(blocks, dim, 0)


def sum_at_owner(x, axis, dim):
    blocks = cut_along(x, dim, lax.axis_size(axis))
    arrived = lax.all_to_all(blocks, axis, split_axis=0, concat_axis=0, tiled=True)
    return arrived.sum(axis=0)


def sum_by_chip(x, chips, core, dim):
    sizes = (lax.axis_size(chips), lax.axis_size(core))
    blocks = cut_along(x, dim, sizes[0] * sizes[1])
    inside = blocks.shape[1:]
    blocks = blocks.reshape(*sizes, *inside).swapaxes(0, 1).reshape(-1, *inside)
    blocks = lax.psum_scatter(blocks, core, scatter_dimension=0, tiled=True)
    return lax.psum_scatter(blocks, chips, scatter_dimension=0, tiled=True)[0]


def contract(first_op, second_op):
    return lax.dot_general(
        first_op, second_op, (((1,), (1,)), ((), ())), preferred_element_type=jnp.float32
    )


def width_list(feature_dim):
    return [feature_dim >> WIDTHS - 1 - nested for nested in range(WIDTHS)]


def scores(first_op, second_op):
    uppers = width_list(first_op.shape[1])
    result = []
    running = jnp.zeros((first_op.shape[0], second_op.shape[0]), jnp.float32)
    lower_col = 0
    for upper_col in uppers:
        running = running + contract(
            first_op[:, lower_col:upper_col], second_op[:, lower_col:upper_col]
        )
        result.append(running * (logit_gain * upper_col ** (-0.5)))
        lower_col = upper_col
    return result


def band_sums(logit_list, total_list, target, uppers):
    bands = [None] * len(uppers)
    running = None
    for nested in reversed(range(len(uppers))):
        scale = logit_gain * uppers[nested] ** (-0.5)
        weight = (jnp.exp(logit_list[nested] - total_list[nested]) - target) * scale
        running = weight if running is None else running + weight
        bands[nested] = running.astype(jnp.bfloat16)
    return bands


def spread(bands, operand, uppers, transposed):
    pieces = []
    lower_col = 0
    for nested, upper_col in enumerate(uppers):
        block_part = operand[:, lower_col:upper_col]
        if transposed:
            product = lax.dot_general(
                bands[nested],
                block_part,
                (((0,), (0,)), ((), ())),
                preferred_element_type=jnp.float32,
            )
        else:
            product = jnp.dot(bands[nested], block_part, preferred_element_type=jnp.float32)
        pieces.append(product)
        lower_col = upper_col
    return jnp.concatenate(pieces, axis=1)


def combine(first_pair, second_pair):
    biggest = jnp.maximum(first_pair[0], second_pair[0])
    return (
        biggest,
        first_pair[1] * jnp.exp(first_pair[0] - biggest)
        + second_pair[1] * jnp.exp(second_pair[0] - biggest),
    )


def on_device(queries, documents, partner):
    own_rows = queries.shape[0]
    uppers = width_list(queries.shape[1])
    rep_index = lax.axis_index("rep")
    rep_count = lax.axis_size("rep")
    pair_rows, pair_partner = (collect(queries, "rep", 0), collect(partner, "rep", 0))
    partner_docs = lax.all_gather(documents, DP, axis=0, tiled=True)
    col_pos = jnp.arange(partner_docs.shape[0], dtype=jnp.int32)
    col_ids = (col_pos // own_rows * rep_count + rep_index) * own_rows + col_pos % own_rows
    target = (pair_partner[:, None] == col_ids[None, :]).astype(jnp.float32)
    logit_list = scores(pair_rows, partner_docs)
    row_peaks = jnp.stack([jnp.max(logits, axis=1) for logits in logit_list])
    masses = jnp.stack(
        [
            jnp.sum(jnp.exp(logits - row_peaks[nested][:, None]), axis=1)
            for nested, logits in enumerate(logit_list)
        ]
    )
    row_peaks, masses = merged((row_peaks, masses), "rep", combine)
    totals = row_peaks + jnp.log(masses)
    bands = band_sums(
        logit_list, [totals[nested][:, None] for nested in range(len(uppers))], target, uppers
    )
    partial_queries = spread(bands, partner_docs, uppers, False)
    grad_queries = sum_at_owner(partial_queries, "rep", 0)
    sliced = [factor for factor in bands]
    grad_documents = sum_by_chip(
        spread(sliced, pair_rows, uppers, True), ("dp_0", "dp_1", "dp_2"), "dp_3", 0
    )
    return (grad_queries, grad_documents)


def solution(mesh):
    finer = Mesh(
        mesh.devices.reshape(4, 2, 4, 2, mesh.shape["rep"]), ("dp_0", "dp_1", "dp_2", "dp_3", "rep")
    )
    placed = (P(DP_REP, None), P(DP_REP, None), P(DP_REP))
    return jax.shard_map(
        on_device,
        mesh=finer,
        in_specs=placed,
        out_specs=(P(DP_REP, None), P(DP_REP, None)),
        check_vma=False,
    )
```

profile of v0, /device:TPU:1, one launch (start us, length us, event | category | flops | bytes accessed | tf_op | source)
XLA Modules:
  0.0 518.1 jit_solution(7170143682551162871)
XLA Ops:
  9.7 5.7 %all-to-all-start = ((bf16[2,64,2048]{2,1,0:T(8,128)(2,1)}), bf16[2,64,2048]{2,1,0:T(8,128)(2,1)S(1)}, u32[]{:S(2)}, u32[]{:S(2)}) async-start(bf16[2,64,2048]{2,1,0:T(8,128)(2,1)} %broadcast_in_dim.10), calls=%async_computation | async-start | bytes 1048576 | tf_op jit(solution)/shard_map/all_to_all | solution.py:23
  15.4 8.6 %all-to-all-done = bf16[2,64,2048]{2,1,0:T(8,128)(2,1)S(1)} async-done(((bf16[2,64,2048]{2,1,0:T(8,128)(2,1)}), bf16[2,64,2048]{2,1,0:T(8,128)(2,1)S(1)}, u32[]{:S(2)}, u32[]{:S(2)}) %all-to-all-start) | async-done | bytes 524320 | tf_op jit(solution)/shard_map/all_to_all | solution.py:23
  24.6 3.2 all-to-all-start.2
  27.8 107.0 %all-gather.2.cloned.1.call-done = bf16[4096,2048]{1,0:T(8,128)(2,1)} async-done(((bf16[64,2048]{1,0:T(8,128)(2,1)}), bf16[4096,2048]{1,0:T(8,128)(2,1)}) %all-gather.2.cloned.1.call-update) | async-done | bytes 16777232 | tf_op jit(solution)/shard_map/all_gather | solution.py:150
  137.1 2.1 multiply_reduce_fusion.6
  142.3 2.1 multiply_reduce_fusion.4
  150.1 2.5 multiply_reduce_fusion.1
  153.1 4.1 multiply_reduce_fusion
  157.7 5.7 %fusion.110 = (f32[128]{0:T(128)S(1)}, f32[128,4096]{1,0:T(8,128)S(1)}) fusion(f32[128,4096]{1,0:T(8,128)S(1)} %get-tuple-element.34, bf16[4096,2048]{1,0:T(8,128)(2,1)} %all-gather.2.cloned.1.call-done, bf16[128,2048]{1,0:T(8,128)(2,1)} %bitcast.69), kind=kOutput, calls=%fused_computation.155 | convolution fusion | flops 1075314560 | bytes 12845568 | tf_op jit(solution)/shard_map/dot_general | solution.py:82
  165.8 4.2 all-to-all-start.1
  171.2 3.1 all-to-all-done.1
  174.4 8.6 %fusion.30 = (bf16[128,4096]{1,0:T(8,128)(2,1)S(1)}, bf16[128,4096]{1,0:T(8,128)(2,1)S(1)}, bf16[128,4096]{1,0:T(8,128)(2,1)S(1)}, bf16[128,4096]{1,0:T(8,128)(2...) fusion(f32[128,4096]{1,0:T(8,128)} %copy-done, ...), kind=kLoop, calls=%fused_computation.51 | loop fusion | flops 27787264 | bytes 27284480 | tf_op jit(solution)/shard_map/convert_element_type | solution.py:112
  191.5 2.7 convolution_dynamic-update-slice_fusion.2
  194.2 4.5 convolution_dynamic-update-slice_fusion.1
  198.7 8.2 %convolution_dynamic-update-slice_fusion = f32[4096,2048]{0,1:T(8,128)} fusion(f32[4096,2048]{0,1:T(8,128)} %convolution_dynamic-update-slice_fusion.1, bf16[128,2048]{1,0:T(8,128)(2,1)S(1)} %bitcast.78, f32[128,4096]{1,0:T(8,128)S(1)} %copy-done.7, s32[4096]{0:T(1024)S(1)} %fusion.95, f32[128]{0:T(128)S(1)} %get-tuple-element.10, s32[128]{0:T(128)S(1)} %eq.17), kind=kOutput, calls=%fused_computation | convolution fusion | flops 1076887552 | bytes 19153920 | tf_op jit(solution)/shard_map/dot_general | solution.py:122
  206.9 33.3 %copy.33 = f32[4096,2048]{1,0:T(8,128)} copy(f32[4096,2048]{0,1:T(8,128)} %convolution_dynamic-update-slice_fusion) | data formatting | bytes 67108864 | tf_op jit(solution)/shard_map/concatenate | solution.py:132
  240.2 23.0 %copy.34 = f32[2,32,64,2048]{3,2,1,0:T(8,128)} copy(f32[2,32,64,2048]{3,2,0,1:T(8,128)} %bitcast.60) | data formatting | bytes 67108864 | tf_op jit(solution)/shard_map/transpose | solution.py:76
  263.5 43.1 %reduce-scatter.3.cloned.1.call-done = f32[32,64,2048]{2,1,0:T(8,128)} async-done(((f32[64,64,2048]{2,1,0:T(8,128)}), f32[32,64,2048]{2,1,0:T(8,128)}) %reduce-scatter.3.cloned.1.call-update) | async-done | bytes 16777232 | tf_op jit(solution)/shard_map/reduce_scatter | solution.py:77
  314.4 2.4 fusion.38
  316.8 2.3 fusion.35
  319.1 2.3 fusion.31
  321.4 2.9 fusion.10
  324.4 4.9 fusion
  329.7 181.0 %all_to_all.21 = f32[2,64,2048]{2,1,0:T(8,128)S(1)} all-to-all(f32[2,64,2048]{2,1,0:T(8,128)S(1)} %bitcast.79), channel_id=1, replica_groups=mesh['dp_0'=4,'dp_1'=2,'dp_2'=4,'dp_3'=2,'rep'=2] {'rep'}, dimensions={0} | all-to-all | bytes 2097152 | tf_op jit(solution)/shard_map/all_to_all | solution.py:68
  (105 shorter events, 36.4 us)
Async XLA Ops:
  7.2 16.8 %copy-start.30 = (s32[64]{0:T(128)S(1)}, s32[64]{0:T(128)}, u32[]{:S(2)}) copy-start(s32[64]{0:T(128)} %param.5) | copy-start | bytes 772
  7.2 127.7 %all-gather.2.cloned.1.call-start = ((), (), s32[]{:S(2)}) async-start(), calls=%async_computation.6 | async-start | bytes 17039360 | tf_op jit(solution)/shard_map/all_gather | solution.py:150
  9.7 14.3 %all-to-all-start = ((bf16[2,64,2048]{2,1,0:T(8,128)(2,1)}), bf16[2,64,2048]{2,1,0:T(8,128)(2,1)S(1)}, u32[]{:S(2)}, u32[]{:S(2)}) async-start(bf16[2,64,2048]{2,1,0:T(8,128)(2,1)} %broadcast_in_dim.10), calls=%async_computation | async-start | bytes 1048576 | tf_op jit(solution)/shard_map/all_to_all | solution.py:23
  24.0 113.1 %copy-start.11 = (bf16[2,64,2048]{2,1,0:T(8,128)(2,1)}, bf16[2,64,2048]{2,1,0:T(8,128)(2,1)S(1)}, u32[]{:S(2)}) copy-start(bf16[2,64,2048]{2,1,0:T(8,128)(2,1)S(1)} %all-to-all-done) | copy-start | bytes 1572868
  24.6 140.6 %all-to-all-start.2 = ((s32[2,1,64]{2,1,0:T(1,128)}), s32[2,1,64]{2,1,0:T(1,128)S(1)}, u32[]{:S(2)}, u32[]{:S(2)}) async-start(s32[2,1,64]{2,1,0:T(1,128)} %broadcast_in_dim.12), calls=%async_computation.2 | async-start | bytes 2048 | tf_op jit(solution)/shard_map/all_to_all | solution.py:23
  152.6 4.6 copy-start.5
  157.2 6.2 %copy-start.8 = (f32[128,4096]{1,0:T(8,128)}, f32[128,4096]{1,0:T(8,128)S(1)}, u32[]{:S(2)}) copy-start(f32[128,4096]{1,0:T(8,128)S(1)} %get-tuple-element.34) | copy-start | bytes 6291460
  165.8 8.5 %all-to-all-start.1 = ((f32[2,18,128]{2,1,0:T(8,128)}), f32[2,18,128]{2,1,0:T(8,128)S(1)}, u32[]{:S(2)}, u32[]{:S(2)}) async-start(f32[2,18,128]{2,1,0:T(8,128)} %broadcast_in_dim.11), calls=%async_computation.1 | async-start | bytes 49152 | tf_op jit(solution)/shard_map/all_to_all | solution.py:23
  170.0 136.6 %reduce-scatter.3.cloned.1.call-start = ((), (), s32[]{:S(2)}) async-start(), calls=%async_computation.7 | async-start | bytes 50331648 | tf_op jit(solution)/shard_map/reduce_scatter | solution.py:77
  171.2 27.4 %copy-start.28 = (s32[128]{0:T(128)}, s32[128]{0:T(128)S(1)}, u32[]{:S(2)}) copy-start(s32[128]{0:T(128)S(1)} %eq.17) | copy-start | bytes 1540
  174.3 24.3 %copy-start.26 = (f32[128]{0:T(128)}, f32[128]{0:T(128)S(1)}, u32[]{:S(2)}) copy-start(f32[128]{0:T(128)S(1)} %get-tuple-element.10) | copy-start | bytes 1540
  174.3 8.7 %copy-start.12 = (bf16[2,64,2048]{2,1,0:T(8,128)(2,1)S(1)}, bf16[2,64,2048]{2,1,0:T(8,128)(2,1)}, u32[]{:S(2)}) copy-start(bf16[2,64,2048]{2,1,0:T(8,128)(2,1)} %copy-done.11) | copy-start | bytes 1572868
  183.0 5.2 %copy-start.17 = (bf16[128,4096]{1,0:T(8,128)(2,1)}, bf16[128,4096]{1,0:T(8,128)(2,1)S(1)}, u32[]{:S(2)}) copy-start(bf16[128,4096]{1,0:T(8,128)(2,1)S(1)} %get-tuple-element.5) | copy-start | bytes 3145732
  183.0 5.2 %copy-start.19 = (bf16[128,4096]{1,0:T(8,128)(2,1)}, bf16[128,4096]{1,0:T(8,128)(2,1)S(1)}, u32[]{:S(2)}) copy-start(bf16[128,4096]{1,0:T(8,128)(2,1)S(1)} %get-tuple-element.4) | copy-start | bytes 3145732
  183.0 5.2 %copy-start.15 = (bf16[128,4096]{1,0:T(8,128)(2,1)}, bf16[128,4096]{1,0:T(8,128)(2,1)S(1)}, u32[]{:S(2)}) copy-start(bf16[128,4096]{1,0:T(8,128)(2,1)S(1)} %get-tuple-element.6) | copy-start | bytes 3145732
  183.0 6.6 %copy-start.13 = (bf16[128,4096]{1,0:T(8,128)(2,1)}, bf16[128,4096]{1,0:T(8,128)(2,1)S(1)}, u32[]{:S(2)}) copy-start(bf16[128,4096]{1,0:T(8,128)(2,1)S(1)} %get-tuple-element.7) | copy-start | bytes 3145732
  183.0 11.1 %copy-start.21 = (bf16[128,4096]{1,0:T(8,128)(2,1)}, bf16[128,4096]{1,0:T(8,128)(2,1)S(1)}, u32[]{:S(2)}) copy-start(bf16[128,4096]{1,0:T(8,128)(2,1)S(1)} %get-tuple-element.3) | copy-start | bytes 3145732
  183.0 11.1 %copy-start.23 = (bf16[128,4096]{1,0:T(8,128)(2,1)}, bf16[128,4096]{1,0:T(8,128)(2,1)S(1)}, u32[]{:S(2)}) copy-start(bf16[128,4096]{1,0:T(8,128)(2,1)S(1)} %get-tuple-element.2) | copy-start | bytes 3145732
  183.1 11.1 %copy-start.9 = (bf16[128,4096]{1,0:T(8,128)(2,1)}, bf16[128,4096]{1,0:T(8,128)(2,1)S(1)}, u32[]{:S(2)}) copy-start(bf16[128,4096]{1,0:T(8,128)(2,1)S(1)} %get-tuple-element.9) | copy-start | bytes 3145732
  194.2 4.5 copy-start.7
  263.3 248.3 %reduce-scatter.5.cloned.1.call-start = ((), (), s32[]{:S(2)}) async-start(), calls=%async_computation.8 | async-start | bytes 17301504 | tf_op jit(solution)/shard_map/reduce_scatter | solution.py:78
  312.5 4.3 copy-start.14
  324.4 4.9 copy-start.24
  324.4 4.9 copy-start.25
  (13 other events, 36.1 us)
Sparse Core Ops, SparseCore 0:
  9.7 125.0 all-gather.1
  263.4 43.1 reduce-scatter.2
  309.6 187.7 reduce-scatter.4
where the time goes:
time: 523 us; the launch traced here: 518 us
  blocking collectives  181 us (35%)
  waiting for transfers between devices  163 us (31%)
  matrix products  70.6 us (13%)
  local copies, waits for them, and re-layouts  61.9 us (12%)
  other arithmetic  14.5 us (3%)
  between operations  14.2 us (3%)
  starting transfers between devices  13.4 us (3%)
    all_to_all x1, blocking collectives, sum_at_owner(): lax.all_to_all(blocks, axis, split_axis=0, concat_axis=0, tiled=True)  181 us
    all_gather x1, waiting for transfers between devices, on_device(): partner_docs = lax.all_gather(documents, DP, axis=0, tiled=True)  107 us
    reduce_scatter x1, waiting for transfers between devices, sum_by_chip(): blocks = lax.psum_scatter(blocks, core, scatter_dimension=0, tiled=True)  43.1 us
    concatenate x2, local copies, waits for them, and re-layouts, spread(): return jnp.concatenate(pieces, axis=1)  33.7 us
    dot_general x9, matrix products, contract(): lax.dot_general(first_op, second_op, (((1,), (1,)), ((), ())), preferred_...  24.4 us
    dot_general x9, matrix products, spread(): lax.dot_general(bands[nested], block_part, (((0,), (0,)), ((), ())), pref...  23.8 us
    transpose x1, local copies, waits for them, and re-layouts, sum_by_chip(): blocks = blocks.reshape(*sizes, *inside).swapaxes(0, 1).reshape(-1, *inside)  23 us
    dot_general x9, matrix products, spread(): jnp.dot(bands[nested], block_part, preferred_element_type=jnp.float32)  22.4 us
  transfers between devices with their start and end apart: 6, of which 4 were waited for; matrix products, arithmetic and copies ran while one was open for 11% of the time, Pallas kernels for 0%

commit v1 on v0

v1 whole, which is shorter than its diff:
```python
import jax
import jax.numpy as jnp
from jax import lax
from jax.sharding import Mesh
from jax.sharding import PartitionSpec as P

WIDTHS = 9
DP = ("dp_0", "dp_1", "dp_2", "dp_3")
DP_REP = ("dp_0", "dp_1", "dp_2", "dp_3", "rep")


logit_gain = 3.0


def contract(first_op, second_op):
    return lax.dot_general(
        first_op, second_op, (((1,), (1,)), ((), ())), preferred_element_type=jnp.float32
    )


def width_list(feature_dim):
    return [feature_dim >> WIDTHS - 1 - nested for nested in range(WIDTHS)]


def scores(first_op, second_op):
    uppers = width_list(first_op.shape[1])
    result = []
    running = jnp.zeros((first_op.shape[0], second_op.shape[0]), jnp.float32)
    lower_col = 0
    for upper_col in uppers:
        running = running + contract(
            first_op[:, lower_col:upper_col], second_op[:, lower_col:upper_col]
        )
        result.append(running * (logit_gain * upper_col ** (-0.5)))
        lower_col = upper_col
    return result


def band_sums(logit_list, total_list, target, uppers):
    bands = [None] * len(uppers)
    running = None
    for nested in reversed(range(len(uppers))):
        scale = logit_gain * uppers[nested] ** (-0.5)
        weight = (jnp.exp(logit_list[nested] - total_list[nested]) - target) * scale
        running = weight if running is None else running + weight
        bands[nested] = running.astype(jnp.bfloat16)
    return bands


def spread(bands, operand, uppers, transposed):
    pieces = []
    lower_col = 0
    for nested, upper_col in enumerate(uppers):
        block_part = operand[:, lower_col:upper_col]
        if transposed:
            product = lax.dot_general(
                bands[nested],
                block_part,
                (((0,), (0,)), ((), ())),
                preferred_element_type=jnp.float32,
            )
        else:
            product = jnp.dot(bands[nested], block_part, preferred_element_type=jnp.float32)
        pieces.append(product)
        lower_col = upper_col
    return jnp.concatenate(pieces, axis=1)


Q_AXES = ("dp_0", "dp_1")
D_AXES = ("dp_2", "dp_3", "rep")


def on_device(queries, documents, partner):
    own_rows = queries.shape[0]
    uppers = width_list(queries.shape[1])
    rows = lax.all_gather(queries, Q_AXES, axis=0, tiled=True)
    row_partner = lax.all_gather(partner, Q_AXES, axis=0, tiled=True)
    docs = lax.all_gather(documents, D_AXES, axis=0, tiled=True)
    x_size, core_size, rep_size = [lax.axis_size(name) for name in D_AXES]
    block = lax.axis_index(Q_AXES)
    shards = block * (x_size * core_size * rep_size)
    col_ids = shards * own_rows + jnp.arange(docs.shape[0], dtype=jnp.int32)
    target = (row_partner[:, None] == col_ids[None, :]).astype(jnp.float32)
    logit_list = scores(rows, docs)
    row_peaks = jnp.stack([jnp.max(logits, axis=1) for logits in logit_list])
    masses = jnp.stack(
        [
            jnp.sum(jnp.exp(logits - row_peaks[nested][:, None]), axis=1)
            for nested, logits in enumerate(logit_list)
        ]
    )
    parts = lax.all_gather(row_peaks + jnp.log(masses), Q_AXES, axis=0)
    peak = jnp.max(parts, axis=0)
    totals = peak + jnp.log(jnp.sum(jnp.exp(parts - peak[None]), axis=0))
    bands = band_sums(
        logit_list, [totals[nested][:, None] for nested in range(len(uppers))], target, uppers
    )
    grad_documents = lax.psum_scatter(
        spread(bands, rows, uppers, True), D_AXES, scatter_dimension=0, tiled=True
    )
    grad_queries = lax.psum_scatter(
        spread(bands, docs, uppers, False), Q_AXES, scatter_dimension=0, tiled=True
    )
    return (grad_queries, grad_documents)


def solution(mesh):
    finer = Mesh(
        mesh.devices.reshape(4, 2, 4, 2, mesh.shape["rep"]), ("dp_0", "dp_1", "dp_2", "dp_3", "rep")
    )
    placed = (P(DP_REP, None), P(DP_REP, None), P(DP_REP))
    return jax.shard_map(
        on_device,
        mesh=finer,
        in_specs=placed,
        out_specs=(P(DP_REP, None), P(DP_REP, None)),
        check_vma=False,
    )
```

time: 523 us -> 407 us (0.78)
  blocking collectives: 181 us -> 32.3 us
  waiting for transfers between devices: 163 us -> 279 us
  local copies, waits for them, and re-layouts: 61.9 us -> 18.7 us
  matrix products: 70.6 us -> 45.7 us
  starting transfers between devices: 13.4 us -> 0.16 us
    all_to_all x1 -> x0, blocking collectives: 181 us -> none  [sum_at_owner(): lax.all_to_all(blocks, axis, split_axis=0, concat_axis=0, tiled=True)]
    unnamed x3 -> x5, waiting for transfers between devices: 0.71 us -> 108 us
    concatenate x2 -> x1, local copies, waits for them, and re-layouts: 33.7 us -> 5.92 us  [spread(): return jnp.concatenate(pieces, axis=1)]
    reduce_scatter x2 -> x1, waiting for transfers between devices: 43.1 us -> 68.8 us  [on_device(): lax.psum_scatter(spread(bands, docs, uppers, False), Q_AXES, scatter_dime...]
    transpose x1 -> x0, local copies, waits for them, and re-layouts: 23 us -> none  [sum_by_chip(): blocks = blocks.reshape(*sizes, *inside).swapaxes(0, 1).reshape(-1, *inside)]
    all_gather x0 -> x1, blocking collectives: none -> 22.3 us  [on_device(): parts = lax.all_gather(row_peaks + jnp.log(masses), Q_AXES, axis=0)]
    all_to_all x3 -> x0, starting transfers between devices: 13.1 us -> none  [copy_for_each(): return lax.all_to_all(copies, axis, split_axis=0, concat_axis=0, tiled=True)]
    all_to_all x3 -> x0, waiting for transfers between devices: 11.7 us -> none  [copy_for_each(): return lax.all_to_all(copies, axis, split_axis=0, concat_axis=0, tiled=True)]
  transfers between devices with their start and end apart: 6 -> 4, of which waited for: 4 -> 4; matrix products, arithmetic and copies ran while one was open for 11% -> 7% of each run, Pallas kernels for 0% -> 0%
where the time goes in v1:
time: 407 us; the launch traced here: 405 us
  waiting for transfers between devices  279 us (69%)
  matrix products  45.7 us (11%)
  blocking collectives  32.3 us (8%)
  local copies, waits for them, and re-layouts  18.7 us (5%)
  between operations  14.7 us (4%)
  other arithmetic  14.4 us (4%)
    unnamed x5, waiting for transfers between devices  108 us
    reduce_scatter x1, waiting for transfers between devices, on_device(): lax.psum_scatter(spread(bands, docs, uppers, False), Q_AXES, scatter_dime...  68.8 us
    all_gather x1, waiting for transfers between devices, on_device(): docs = lax.all_gather(documents, D_AXES, axis=0, tiled=True)  61.3 us
    all_gather x1, waiting for transfers between devices, on_device(): rows = lax.all_gather(queries, Q_AXES, axis=0, tiled=True)  41.1 us
    all_gather x1, blocking collectives, on_device(): parts = lax.all_gather(row_peaks + jnp.log(masses), Q_AXES, axis=0)  22.3 us
    dot_general x9, matrix products, contract(): lax.dot_general(first_op, second_op, (((1,), (1,)), ((), ())), preferred_...  18.1 us
    dot_general x9, matrix products, spread(): lax.dot_general(bands[nested], block_part, (((0,), (0,)), ((), ())), pref...  16.7 us
    unnamed x54, local copies, waits for them, and re-layouts  12.7 us
  transfers between devices with their start and end apart: 4, of which 4 were waited for; matrix products, arithmetic and copies ran while one was open for 7% of the time, Pallas kernels for 0%

profile of v1, /device:TPU:1, one launch (start us, length us, event | category | flops | bytes accessed | tf_op | source)
XLA Modules:
  0.0 405.3 jit_solution(15997544416432338773)
XLA Ops:
  11.5 10.0 %all-reduce = s32[512]{0:T(512)S(1)} all-reduce(s32[512]{0:T(512)S(1)} %dynamic-update-slice), channel_id=1, replica_groups=mesh['dp_0'=4,'dp_1'=2,'dp_2'=4,'dp_3'=2,'rep'=2] {'dp_0','dp_1'}, use_global_device_ids=true, to_apply=%add | all-reduce | flops 512 | bytes 4096
  21.5 41.1 %all-gather.3.cloned.1.call-done = bf16[512,2048]{1,0:T(8,128)(2,1)} async-done(((bf16[64,2048]{1,0:T(8,128)(2,1)}), bf16[512,2048]{1,0:T(8,128)(2,1)}) %all-gather.3.cloned.1.call-update) | async-done | bytes 2097168 | tf_op jit(solution)/shard_map/all_gather | solution.py:76
  62.6 61.3 %all-gather.5.cloned.1.call-done = bf16[1024,2048]{1,0:T(8,128)(2,1)} async-done(((bf16[64,2048]{1,0:T(8,128)(2,1)}), bf16[1024,2048]{1,0:T(8,128)(2,1)}) %all-gather.5.cloned.1.call-update) | async-done | bytes 4194320 | tf_op jit(solution)/shard_map/all_gather | solution.py:78
  123.9 1.5 multiply_reduce_fusion.7
  125.9 1.6 multiply_reduce_fusion.6
  128.1 1.8 multiply_reduce_fusion.5
  130.5 1.8 multiply_reduce_fusion.4
  132.8 1.8 multiply_reduce_fusion.3
  135.2 1.7 multiply_reduce_fusion.2
  137.4 1.9 multiply_reduce_fusion.1
  139.9 2.4 multiply_reduce_fusion
  142.8 3.5 fusion.92
  148.3 22.3 %all_gather.15 = f32[8,9,512]{2,1,0:T(8,128)S(1)} all-gather(f32[1,9,512]{2,1,0:T(8,128)S(1)} %log_add_fusion.1), channel_id=1, replica_groups=mesh['dp_0'=4,'dp_1'=2,'dp_2'=4,'dp_3'=2,'rep'=2] {'dp_0','dp_1'}, dimensions={0}, use_global_device_ids=true | all-gather | bytes 165888 | tf_op jit(solution)/shard_map/all_gather | solution.py:92
  170.8 9.6 %fusion.17 = (bf16[512,1024]{1,0:T(8,128)(2,1)S(1)}, bf16[512,1024]{1,0:T(8,128)(2,1)S(1)}, bf16[512,1024]{1,0:T(8,128)(2,1)S(1)}, bf16[512,1024]{1,0:T(8,128)(2...) fusion(f32[512,1024]{1,0:T(8,128)S(1)} %get-tuple-element.24, ...), kind=kLoop, calls=%fused_computation.27 | loop fusion | flops 27787264 | bytes 27287552 | tf_op jit(solution)/shard_map/convert_element_type | solution.py:46
  189.7 1.7 fusion.27
  191.4 5.9 %concatenate.20 = f32[512,2048]{1,0:T(8,128)} concatenate(f32[512,8]{1,0:T(8,128)S(1)} %fusion.66, f32[512,8]{1,0:T(8,128)} %fusion.48, f32[512,16]{1,0:T(8,128)} %fusion.45, f32[512,32]{1,0:T(8,128)} %fusion.42, f32[512,64]{1,0:T(8,128)} %fusion.39, f32[512,128]{1,0:T(8,128)} %fusion.36, f32[512,256]{1,0:T(8,128)} %fusion.33, f32[512,512]{1,0:T(8,128)} %fusion.27, ...), dimensions={1} | concatenate | bytes 8388608 | tf_op jit(solution)/shard_map/concatenate | solution.py:66
  197.4 2.3 convolution_dynamic-update-slice_fusion.8
  199.7 2.0 convolution_dynamic-update-slice_fusion.7
  201.7 2.0 convolution_dynamic-update-slice_fusion.6
  208.5 2.1 convolution_dynamic-update-slice_fusion.1
  210.6 3.5 convolution_dynamic-update-slice_fusion
  214.1 9.1 %copy.31 = f32[1024,2048]{1,0:T(8,128)} copy(f32[1024,2048]{0,1:T(8,128)} %convolution_dynamic-update-slice_fusion) | data formatting | bytes 16777216
  223.3 68.8 %reduce-scatter.5.cloned.1.call-done = f32[64,2048]{1,0:T(8,128)} async-done(((f32[512,2048]{1,0:T(8,128)}), f32[64,2048]{1,0:T(8,128)}) %reduce-scatter.5.cloned.1.call-update) | async-done | bytes 524304 | tf_op jit(solution)/shard_map/reduce_scatter | solution.py:101
  292.0 106.8 %reduce-scatter.7.cloned.1.call-done = f32[64,2048]{1,0:T(8,128)} async-done(((f32[1024,2048]{1,0:T(8,128)}), f32[64,2048]{1,0:T(8,128)}) %reduce-scatter.7.cloned.1.call-update) | async-done | bytes 524304
  (90 shorter events, 24.1 us)
Async XLA Ops:
  7.2 55.4 %all-gather.3.cloned.1.call-start = ((), (), s32[]{:S(2)}) async-start(), calls=%async_computation.2 | async-start | bytes 2359296 | tf_op jit(solution)/shard_map/all_gather | solution.py:76
  7.9 116.0 %all-gather.5.cloned.1.call-start = ((), (), s32[]{:S(2)}) async-start(), calls=%async_computation.3 | async-start | bytes 4456448 | tf_op jit(solution)/shard_map/all_gather | solution.py:78
  8.6 283.4 %reduce-scatter.5.cloned.1.call-start = ((), (), s32[]{:S(2)}) async-start(), calls=%async_computation.4 | async-start | bytes 4718592 | tf_op jit(solution)/shard_map/reduce_scatter | solution.py:101
  127.6 2.4 copy-start
  129.9 2.4 copy-start.1
  132.3 2.4 copy-start.2
  136.9 2.4 copy-start.4
  139.3 3.0 copy-start.5
  142.3 4.0 copy-start.6
  170.7 9.7 %copy-start.17 = (f32[512,1024]{1,0:T(8,128)S(1)}, f32[512,1024]{1,0:T(8,128)}, u32[]{:S(2)}) copy-start(f32[512,1024]{1,0:T(8,128)} %copy-done.16) | copy-start | bytes 6291460
  170.7 9.7 %copy-start.19 = (bf16[1024,2048]{1,0:T(8,128)(2,1)S(1)}, bf16[1024,2048]{1,0:T(8,128)(2,1)}, u32[]{:S(2)}) copy-start(bf16[1024,2048]{1,0:T(8,128)(2,1)} %all-gather.5.cloned.1.call-done) | copy-start | bytes 12582916
  180.4 3.2 copy-start.11
  180.5 5.6 %copy-start.9 = (bf16[512,1024]{1,0:T(8,128)(2,1)}, bf16[512,1024]{1,0:T(8,128)(2,1)S(1)}, u32[]{:S(2)}) copy-start(bf16[512,1024]{1,0:T(8,128)(2,1)S(1)} %get-tuple-element.10) | copy-start | bytes 3145732
  180.5 6.8 %copy-start.7 = (bf16[512,1024]{1,0:T(8,128)(2,1)}, bf16[512,1024]{1,0:T(8,128)(2,1)S(1)}, u32[]{:S(2)}) copy-start(bf16[512,1024]{1,0:T(8,128)(2,1)S(1)} %get-tuple-element.11) | copy-start | bytes 3145732
  180.5 8.0 %copy-start.23 = (bf16[512,1024]{1,0:T(8,128)(2,1)}, bf16[512,1024]{1,0:T(8,128)(2,1)S(1)}, u32[]{:S(2)}) copy-start(bf16[512,1024]{1,0:T(8,128)(2,1)S(1)} %get-tuple-element.12) | copy-start | bytes 3145732
  180.5 9.2 %copy-start.21 = (bf16[512,1024]{1,0:T(8,128)(2,1)}, bf16[512,1024]{1,0:T(8,128)(2,1)S(1)}, u32[]{:S(2)}) copy-start(bf16[512,1024]{1,0:T(8,128)(2,1)S(1)} %get-tuple-element.13) | copy-start | bytes 3145732
  197.3 2.4 copy-start.14
  197.4 4.3 %copy-start.12 = (bf16[512,1024]{1,0:T(8,128)(2,1)S(1)}, bf16[512,1024]{1,0:T(8,128)(2,1)}, u32[]{:S(2)}) copy-start(bf16[512,1024]{1,0:T(8,128)(2,1)} %copy-done.11) | copy-start | bytes 3145732
  197.4 201.4 %reduce-scatter.7.cloned.1.call-start = ((), (), s32[]{:S(2)}) async-start(), calls=%async_computation.5 | async-start | bytes 8912896
  197.4 6.2 %copy-start.20 = (bf16[512,2048]{1,0:T(8,128)(2,1)S(1)}, bf16[512,2048]{1,0:T(8,128)(2,1)}, u32[]{:S(2)}) copy-start(bf16[512,2048]{1,0:T(8,128)(2,1)} %all-gather.3.cloned.1.call-done) | copy-start | bytes 6291460
  199.7 5.0 %copy-start.10 = (bf16[512,1024]{1,0:T(8,128)(2,1)S(1)}, bf16[512,1024]{1,0:T(8,128)(2,1)}, u32[]{:S(2)}) copy-start(bf16[512,1024]{1,0:T(8,128)(2,1)} %copy-done.9) | copy-start | bytes 3145732
  201.7 4.1 %copy-start.8 = (bf16[512,1024]{1,0:T(8,128)(2,1)S(1)}, bf16[512,1024]{1,0:T(8,128)(2,1)}, u32[]{:S(2)}) copy-start(bf16[512,1024]{1,0:T(8,128)(2,1)} %copy-done.7) | copy-start | bytes 3145732
  203.6 3.3 copy-start.24
  205.8 2.7 copy-start.22
  (5 other events, 9.1 us)
Sparse Core Ops, SparseCore 0:
  9.6 52.9 all-gather.2
  65.0 58.8 all-gather.4
  197.5 94.4 reduce-scatter.4
  296.8 101.9 reduce-scatter.6

commit v2 on v1

v2 whole, which is shorter than its diff:
```python
import functools
import jax
import jax.numpy as jnp
from jax import lax
from jax.experimental import pallas as pl
from jax.experimental.pallas import tpu as pltpu
from jax.sharding import Mesh
from jax.sharding import PartitionSpec as P

WIDTHS = 9
logit_gain = 3.0


def contract(first_op, second_op):
    return lax.dot_general(
        first_op, second_op, (((1,), (1,)), ((), ())), preferred_element_type=jnp.float32
    )


def width_list(feature_dim):
    return [feature_dim >> WIDTHS - 1 - nested for nested in range(WIDTHS)]


def scores(first_op, second_op):
    uppers = width_list(first_op.shape[1])
    result = []
    running = jnp.zeros((first_op.shape[0], second_op.shape[0]), jnp.float32)
    lower_col = 0
    for upper_col in uppers:
        running = running + contract(
            first_op[:, lower_col:upper_col], second_op[:, lower_col:upper_col]
        )
        result.append(running * (logit_gain * upper_col ** (-0.5)))
        lower_col = upper_col
    return result


def band_sums(logit_list, total_list, target, uppers):
    bands = [None] * len(uppers)
    running = None
    for nested in reversed(range(len(uppers))):
        scale = logit_gain * uppers[nested] ** (-0.5)
        weight = (jnp.exp(logit_list[nested] - total_list[nested]) - target) * scale
        running = weight if running is None else running + weight
        bands[nested] = running.astype(jnp.bfloat16)
    return bands


def spread(bands, operand, uppers, transposed):
    pieces = []
    lower_col = 0
    for nested, upper_col in enumerate(uppers):
        block_part = operand[:, lower_col:upper_col]
        if transposed:
            product = lax.dot_general(
                bands[nested],
                block_part,
                (((0,), (0,)), ((), ())),
                preferred_element_type=jnp.float32,
            )
        else:
            product = jnp.dot(bands[nested], block_part, preferred_element_type=jnp.float32)
        pieces.append(product)
        lower_col = upper_col
    return jnp.concatenate(pieces, axis=1)


AXES = ("y", "zl", "x", "core", "zh")
MESH = pl.DeviceIdType.MESH
VMEM = pl.BlockSpec(memory_space=pltpu.VMEM)


def neighbours(axis):
    size = lax.axis_size(axis)
    me = lax.axis_index(axis)
    up = {axis: lax.rem(me + 1, size)}
    down = {axis: lax.rem(me + size - 1, size)}
    pair = {"zl": 1 - lax.axis_index("zl")}
    if axis == "x":
        pair["zh"] = 1 - lax.axis_index("zh")
    return up, down, pair


def meet(devices):
    barrier = pltpu.get_barrier_semaphore()
    for device in devices:
        pl.semaphore_signal(barrier, inc=1, device_id=device, device_id_type=MESH)
    pl.semaphore_wait(barrier, len(devices))


def gather_kernel(q_ref, d_ref, rows_ref, docs_ref, sent, landed):
    own = q_ref.shape[0]
    half = own // 2
    sibling = {"core": 1 - lax.axis_index("core")}
    y_up, y_down, y_pair = neighbours("y")
    x_up, x_down, x_pair = neighbours("x")
    meet((y_up, y_down, y_pair, x_up, x_down, x_pair, sibling))
    started = []
    across = []

    def send(src, dst, number, device):
        copy = pltpu.make_async_remote_copy(
            src_ref=src,
            dst_ref=dst,
            send_sem=sent.at[number],
            recv_sem=landed.at[number],
            device_id=device,
            device_id_type=MESH,
        )
        copy.start()
        started.append(copy)
        return copy

    def q_slot(step, pair, lo=0, count=own):
        return rows_ref.at[pl.ds((step * 2 + pair) * own + lo, count), :]

    def d_slot(step, pair, other=0, lo=0, count=own):
        return docs_ref.at[pl.ds(((step * 2 + pair) * 2 + other) * own + lo, count), :]

    lanes = (
        (q_ref, q_slot, y_up, y_down, y_pair, 0),
        (d_ref, d_slot, x_up, x_down, x_pair, 9),
    )
    first = []
    for src, slot, up, down, pair, base in lanes:
        first.append(
            (
                send(src, slot(0, 1), base, pair),
                send(src, slot(3, 0), base + 1, up),
                send(src, slot(1, 0), base + 2, down),
            )
        )
    across.append(send(d_ref, d_slot(0, 0, 1), 18, sibling))
    rows_ref[pl.ds(0, own), :] = q_ref[...]
    docs_ref[pl.ds(0, own), :] = d_ref[...]

    second = []
    for (src, slot, up, down, pair, base), copies in zip(lanes, first):
        copies[0].wait_recv()
        second.append(
            (
                send(slot(0, 1), slot(3, 1), base + 3, up),
                send(slot(0, 1), slot(1, 1), base + 4, down),
            )
        )
    across.append(send(d_slot(0, 1), d_slot(0, 1, 1), 19, sibling))
    far = []
    for (src, slot, up, down, pair, base), copies in zip(lanes, first):
        copies[1].wait_recv()
        far.append(send(slot(3, 0, lo=0, count=half), slot(2, 0, lo=0, count=half), base + 5, up))
        copies[2].wait_recv()
        far.append(
            send(slot(1, 0, lo=half, count=half), slot(2, 0, lo=half, count=half), base + 6, down)
        )
    across.append(send(d_slot(3, 0), d_slot(3, 0, 1), 20, sibling))
    across.append(send(d_slot(1, 0), d_slot(1, 0, 1), 21, sibling))
    for (src, slot, up, down, pair, base), copies in zip(lanes, second):
        copies[0].wait_recv()
        far.append(send(slot(3, 1, lo=0, count=half), slot(2, 1, lo=0, count=half), base + 7, up))
        copies[1].wait_recv()
        far.append(
            send(slot(1, 1, lo=half, count=half), slot(2, 1, lo=half, count=half), base + 8, down)
        )
    across.append(send(d_slot(3, 1), d_slot(3, 1, 1), 22, sibling))
    across.append(send(d_slot(1, 1), d_slot(1, 1, 1), 23, sibling))
    for copy in far:
        copy.wait_recv()
    across.append(send(d_slot(2, 0), d_slot(2, 0, 1), 24, sibling))
    across.append(send(d_slot(2, 1), d_slot(2, 1, 1), 25, sibling))
    for copy in across:
        copy.wait_recv()
    for copy in started:
        copy.wait_send()


def gather(queries, documents):
    own, wide = queries.shape
    return pl.pallas_call(
        gather_kernel,
        out_shape=(
            jax.ShapeDtypeStruct((8 * own, wide), queries.dtype),
            jax.ShapeDtypeStruct((16 * own, documents.shape[1]), documents.dtype),
        ),
        in_specs=[VMEM] * 2,
        out_specs=(VMEM, VMEM),
        scratch_shapes=[pltpu.SemaphoreType.DMA((26,)), pltpu.SemaphoreType.DMA((26,))],
        compiler_params=pltpu.CompilerParams(collective_id=0, has_side_effects=True),
        name="gather",
    )(queries, documents)


def reduce_kernel(pq_ref, pd_ref, gq_ref, gd_ref, sib, far_s, near_s, far_r, near_r, pair_s, pair_r, sent, landed):
    own = gq_ref.shape[0]
    half = own // 2
    sibling = {"core": 1 - lax.axis_index("core")}
    y_up, y_down, y_pair = neighbours("y")
    x_up, x_down, x_pair = neighbours("x")
    meet((y_up, y_down, y_pair, x_up, x_down, x_pair, sibling))
    started = []

    def send(src, dst, number, device):
        copy = pltpu.make_async_remote_copy(
            src_ref=src,
            dst_ref=dst,
            send_sem=sent.at[number],
            recv_sem=landed.at[number],
            device_id=device,
            device_id_type=MESH,
        )
        copy.start()
        started.append(copy)
        return copy

    def q_part(step, pair, lo=0, count=own):
        return pq_ref[pl.ds((step * 2 + pair) * own + lo, count), :]

    across = {}
    for place, (step, pair) in enumerate(
        ((2, 1), (2, 0), (1, 1), (3, 1), (1, 0), (3, 0), (0, 1), (0, 0))
    ):
        src = pd_ref.at[pl.ds(((step * 2 + pair) * 2 + 1) * own, own), :]
        across[step, pair] = send(src, sib.at[step * 2 + pair], 22 + place, sibling)

    def d_part(step, pair, lo=0, count=own):
        mine = pd_ref[pl.ds((step * 2 + pair) * 2 * own + lo, count), :]
        return mine + sib[step * 2 + pair, pl.ds(lo, count), :]

    lanes = ((q_part, y_up, y_down, y_pair), (d_part, x_up, x_down, x_pair))
    far = {}
    for pair in (1, 0):
        for side, (part, up, down, _) in enumerate(lanes):
            if side == 1:
                across[2, pair].wait_recv()
            far_s[side, pair] = part(2, pair).astype(jnp.bfloat16)
            for way, device in ((0, up), (1, down)):
                rows = pl.ds(way * half, half)
                far[side, pair, way] = send(
                    far_s.at[side, pair, rows],
                    far_r.at[side, pair, rows],
                    (side * 2 + pair) * 2 + way,
                    device,
                )
    near = {}
    for pair in (1, 0):
        for side, (part, up, down, _) in enumerate(lanes):
            for way, device, step in ((0, up, 1), (1, down, 3)):
                if side == 1:
                    across[step, pair].wait_recv()
                far[side, pair, way].wait_recv()
                lo = way * half
                more = half - lo
                near_s[side, pair, way, pl.ds(lo, half), :] = (
                    part(step, pair, lo, half)
                    + far_r[side, pair, pl.ds(lo, half), :].astype(jnp.float32)
                ).astype(jnp.bfloat16)
                near_s[side, pair, way, pl.ds(more, half), :] = part(
                    step, pair, more, half
                ).astype(jnp.bfloat16)
                near[side, pair, way] = send(
                    near_s.at[side, pair, way],
                    near_r.at[side, pair, way],
                    8 + (side * 2 + pair) * 2 + way,
                    device,
                )

    def total(side, pair, part):
        if side == 1:
            across[0, pair].wait_recv()
        near[side, pair, 0].wait_recv()
        near[side, pair, 1].wait_recv()
        return (
            part(0, pair)
            + near_r[side, pair, 0].astype(jnp.float32)
            + near_r[side, pair, 1].astype(jnp.float32)
        )

    last = []
    for side, (part, _, _, device) in enumerate(lanes):
        pair_s[side] = total(side, 1, part).astype(jnp.bfloat16)
        last.append(send(pair_s.at[side], pair_r.at[side], 16 + side, device))
    for side, (part, _, _, _) in enumerate(lanes):
        out = (gq_ref, gd_ref)[side]
        out[...] = total(side, 0, part)
    for side in range(2):
        out = (gq_ref, gd_ref)[side]
        last[side].wait_recv()
        out[...] = out[...] + pair_r[side].astype(jnp.float32)
    for copy in started:
        copy.wait_send()


def reduce(part_queries, part_documents):
    own = part_queries.shape[0] // 8
    dim = part_queries.shape[1]
    piece = jax.ShapeDtypeStruct((own, dim), jnp.float32)
    wire = jnp.bfloat16
    return pl.pallas_call(
        reduce_kernel,
        out_shape=(piece, piece),
        in_specs=[VMEM] * 2,
        out_specs=(VMEM, VMEM),
        scratch_shapes=[
            pltpu.VMEM((8, own, dim), jnp.float32),
            pltpu.VMEM((2, 2, own, dim), wire),
            pltpu.VMEM((2, 2, 2, own, dim), wire),
            pltpu.VMEM((2, 2, own, dim), wire),
            pltpu.VMEM((2, 2, 2, own, dim), wire),
            pltpu.VMEM((2, own, dim), wire),
            pltpu.VMEM((2, own, dim), wire),
            pltpu.SemaphoreType.DMA((30,)),
            pltpu.SemaphoreType.DMA((30,)),
        ],
        compiler_params=pltpu.CompilerParams(
            collective_id=1, has_side_effects=True, vmem_limit_bytes=60 * 2**20
        ),
        name="reduce",
    )(part_queries, part_documents)


def totals_kernel(lse_ref, out_ref, parts, sent, landed):
    chips = lax.axis_size("y")
    y = lax.axis_index("y")
    zl = lax.axis_index("zl")
    peers = []
    for step in range(chips):
        for pair in range(2):
            if step or pair:
                peers.append(
                    (step, pair, {"y": lax.rem(y + step, chips), "zl": lax.rem(zl + pair, 2)})
                )
    meet([device for _, _, device in peers])
    copies = []
    for number, (step, pair, device) in enumerate(peers):
        back = (chips - step) % chips
        copy = pltpu.make_async_remote_copy(
            src_ref=lse_ref,
            dst_ref=parts.at[back * 2 + pair],
            send_sem=sent.at[number],
            recv_sem=landed.at[back * 2 + pair],
            device_id=device,
            device_id_type=MESH,
        )
        copy.start()
        copies.append(copy)
    mine = lse_ref[...]
    for copy in copies:
        copy.wait()
    group = mine.shape[1] // chips

    def aligned(step, pair, place):
        if step == 0 and pair == 0:
            return mine[:, place * group : (place + 1) * group]
        at = (place - step) % chips * group
        piece = parts[step * 2 + pair, :, at : at + group]
        return pltpu.roll(piece, group // 2, 1) if pair else piece

    for place in range(chips):
        pieces = [aligned(step, pair, place) for step in range(chips) for pair in range(2)]
        peak = functools.reduce(jnp.maximum, pieces)
        mass = sum(jnp.exp(piece - peak) for piece in pieces)
        out_ref[:, place * group : (place + 1) * group] = peak + jnp.log(mass)


def combined_totals(lse):
    return pl.pallas_call(
        totals_kernel,
        out_shape=jax.ShapeDtypeStruct(lse.shape, jnp.float32),
        in_specs=[VMEM],
        out_specs=VMEM,
        scratch_shapes=[
            pltpu.VMEM((8, *lse.shape), jnp.float32),
            pltpu.SemaphoreType.DMA((8,)),
            pltpu.SemaphoreType.DMA((8,)),
        ],
        compiler_params=pltpu.CompilerParams(collective_id=2, has_side_effects=True),
        name="totals",
    )(lse)


def row_ids(own):
    y, zl, x, core, zh = [lax.axis_index(axis) for axis in AXES]
    chips = lax.axis_size("x")
    ids = []
    for step in range(chips):
        for pair in range(2):
            for other in range(2):
                there_x = lax.rem(x + step, chips)
                there_zl = lax.rem(zl + pair, 2)
                there_zh = lax.rem(zh + pair, 2)
                there_core = lax.rem(core + other, 2)
                chip = (y * 2 + there_zl) * chips + there_x
                shard = (chip * 2 + there_core) * 2 + there_zh
                ids.append(shard * own + jnp.arange(own, dtype=jnp.int32))
    return jnp.concatenate(ids)


def on_device(queries, documents, partner):
    own, dim = queries.shape
    uppers = width_list(dim)
    index = partner.astype(jnp.float32)
    high = jnp.floor(index / 128.0)
    low = index - 128.0 * high
    lane = jnp.arange(128)[None]
    extra = jnp.where(lane == 0, high[:, None], jnp.where(lane == 1, low[:, None], 0.0))
    rows, docs = gather(jnp.concatenate([queries, extra.astype(jnp.bfloat16)], axis=1), documents)
    marks = rows[:, dim : dim + 2].astype(jnp.float32)
    row_partner = (marks[:, 0] * 128.0 + marks[:, 1]).astype(jnp.int32)
    rows = rows[:, :dim]
    target = (row_partner[:, None] == row_ids(own)[None, :]).astype(jnp.float32)
    logit_list = scores(rows, docs)
    row_peaks = jnp.stack([jnp.max(logits, axis=1) for logits in logit_list])
    masses = jnp.stack(
        [
            jnp.sum(jnp.exp(logits - row_peaks[nested][:, None]), axis=1)
            for nested, logits in enumerate(logit_list)
        ]
    )
    lse = jnp.pad(row_peaks + jnp.log(masses), ((0, 16 - WIDTHS), (0, 0)))
    totals = combined_totals(lse)
    bands = band_sums(
        logit_list, [totals[nested][:, None] for nested in range(len(uppers))], target, uppers
    )
    return reduce(spread(bands, docs, uppers, False), spread(bands, rows, uppers, True))


def solution(mesh):
    finer = Mesh(mesh.devices.reshape(4, 2, 4, 2, mesh.shape["rep"]), AXES)
    placed = (P(AXES, None), P(AXES, None), P(AXES))
    return jax.shard_map(
        on_device,
        mesh=finer,
        in_specs=placed,
        out_specs=(P(AXES, None), P(AXES, None)),
        check_vma=False,
    )
```

time: 407 us -> 170 us (0.42)
  waiting for transfers between devices: 279 us -> 0 us
  Pallas kernels: 0 us -> 76 us
  blocking collectives: 32.3 us -> 0 us
  between operations: 14.7 us -> 0.97 us
  matrix products: 45.7 us -> 51.5 us
    unnamed x5 -> x0, waiting for transfers between devices: 108 us -> none
    all_gather x2 -> x0, waiting for transfers between devices: 102 us -> none  [the longest x1 61.3 us: on_device(): docs = lax.all_gather(documents, D_AXES, axis=0, tiled=True)]
    pallas_call x0 -> x3, Pallas kernels: none -> 76 us  [the longest x1 34 us: gather(): pl.pallas_call(gather_kernel, out_shape=(jax.ShapeDtypeStruct((8 * own, w...]
    reduce_scatter x1 -> x0, waiting for transfers between devices: 68.8 us -> none  [on_device(): lax.psum_scatter(spread(bands, docs, uppers, False), Q_AXES, scatter_dime...]
    all_gather x1 -> x0, blocking collectives: 22.3 us -> none  [on_device(): parts = lax.all_gather(row_peaks + jnp.log(masses), Q_AXES, axis=0)]
    unnamed x1 -> x0, blocking collectives: 10 us -> none
    concatenate x1 -> x2, local copies, waits for them, and re-layouts: 5.92 us -> 15.8 us  [spread(): return jnp.concatenate(pieces, axis=1)]
    unnamed x54 -> x26, local copies, waits for them, and re-layouts: 12.7 us -> 5.09 us
  transfers between devices with their start and end apart: 4 -> 0, of which waited for: 4 -> 0; matrix products, arithmetic and copies ran while one was open for 7% -> 0% of each run, Pallas kernels for 0% -> 0%
where the time goes in v2:
time: 170 us; the launch traced here: 169 us
  Pallas kernels  76 us (45%)
  matrix products  51.5 us (30%)
  local copies, waits for them, and re-layouts  22.7 us (13%)
  other arithmetic  17.7 us (10%)
    pallas_call x1, Pallas kernels, gather(): pl.pallas_call(gather_kernel, out_shape=(jax.ShapeDtypeStruct((8 * own, w...  34 us
    pallas_call x1, Pallas kernels, reduce(): pl.pallas_call(reduce_kernel, out_shape=(piece, piece), in_specs=[VMEM] *...  32.9 us
    dot_general x9, matrix products, spread(): lax.dot_general(bands[nested], block_part, (((0,), (0,)), ((), ())), pref...  22.4 us
    dot_general x9, matrix products, contract(): lax.dot_general(first_op, second_op, (((1,), (1,)), ((), ())), preferred_...  18.2 us
    concatenate x2, local copies, waits for them, and re-layouts, spread(): return jnp.concatenate(pieces, axis=1)  15.8 us
    dot_general x9, matrix products, spread(): jnp.dot(bands[nested], block_part, preferred_element_type=jnp.float32)  10.9 us
    convert_element_type x1, other arithmetic, band_sums(): bands[nested] = running.astype(jnp.bfloat16)  9.44 us
    pallas_call x1, Pallas kernels, combined_totals(): pl.pallas_call(totals_kernel, out_shape=jax.ShapeDtypeStruct(lse.shape, j...  9.04 us

profile of v2, /device:TPU:1, one launch (start us, length us, event | category | flops | bytes accessed | tf_op | source)
XLA Modules:
  0.0 168.8 jit_solution(638100238806685752)
XLA Ops:
  3.3 34.0 %gather.1 = (bf16[512,2176]{1,0:T(8,128)(2,1)}, bf16[1024,2048]{1,0:T(8,128)(2,1)}) custom-call(bf16[64,2176]{1,0:T(8,128)(2,1)} %pad_maximum_fusion.q_ref, bf16[64,2048]{1,0:T(8,128)(2,1)} %d_ref.1), custom_call_target="tpu_custom_call" | custom-call | tf_op jit(solution)/shard_map/gather/pallas_call | solution.py:178
  42.7 1.8 %multiply_reduce_fusion.5 = (f32[512]{0:T(512)S(1)}, f32[512,1024]{1,0:T(8,128)S(1)}) fusion(f32[512,1024]{1,0:T(8,128)S(1)} %get-tuple-element.28, bf16[1024,2048]{1,0:T(8,128)(2,1)} %get-tuple-element.5, bf16[512,2176]{1,0:T(8,128)(2,1)} %get-tuple-element.4), kind=kOutput, calls=%fused_computation.42 | convolution fusion | flops 18349568 | bytes 4589568 | tf_op jit(solution)/shard_map/dot_general | solution.py:15
  45.0 1.8 %multiply_reduce_fusion.4 = (f32[512]{0:T(512)S(1)}, f32[512,1024]{1,0:T(8,128)S(1)}) fusion(f32[512,1024]{1,0:T(8,128)S(1)} %get-tuple-element.30, bf16[1024,2048]{1,0:T(8,128)(2,1)} %get-tuple-element.5, bf16[512,2176]{1,0:T(8,128)(2,1)} %get-tuple-element.4), kind=kOutput, calls=%fused_computation.41 | convolution fusion | flops 35126784 | bytes 4589568 | tf_op jit(solution)/shard_map/dot_general | solution.py:15
  47.4 1.8 %multiply_reduce_fusion.3 = (f32[512]{0:T(512)S(1)}, f32[512,1024]{1,0:T(8,128)S(1)}) fusion(f32[512,1024]{1,0:T(8,128)S(1)} %get-tuple-element.32, bf16[1024,2048]{1,0:T(8,128)(2,1)} %get-tuple-element.5, bf16[512,2176]{1,0:T(8,128)(2,1)} %get-tuple-element.4), kind=kOutput, calls=%fused_computation.40 | convolution fusion | flops 68681216 | bytes 4589568 | tf_op jit(solution)/shard_map/dot_general | solution.py:15
  49.7 1.7 %multiply_reduce_fusion.2 = (f32[512]{0:T(512)S(1)}, f32[512,1024]{1,0:T(8,128)S(1)}) fusion(f32[512,1024]{1,0:T(8,128)S(1)} %get-tuple-element.34, bf16[1024,2048]{1,0:T(8,128)(2,1)} %get-tuple-element.5, bf16[512,2176]{1,0:T(8,128)(2,1)} %get-tuple-element.4), kind=kOutput, calls=%fused_computation.39 | convolution fusion | flops 135790080 | bytes 4589568 | tf_op jit(solution)/shard_map/dot_general | solution.py:15
  52.0 1.9 %multiply_reduce_fusion.1 = (f32[512]{0:T(512)S(1)}, f32[512,1024]{1,0:T(8,128)S(1)}) fusion(f32[512,1024]{1,0:T(8,128)S(1)} %get-tuple-element.36, bf16[1024,2048]{1,0:T(8,128)(2,1)} %get-tuple-element.5, bf16[512,2176]{1,0:T(8,128)(2,1)} %get-tuple-element.4), kind=kOutput, calls=%fused_computation.38 | convolution fusion | flops 270007808 | bytes 4982784 | tf_op jit(solution)/shard_map/dot_general | solution.py:15
  54.4 2.4 %multiply_reduce_fusion = (f32[512]{0:T(512)S(1)}, f32[512,1024]{1,0:T(8,128)S(1)}) fusion(f32[512,1024]{1,0:T(8,128)S(1)} %get-tuple-element.38, bf16[1024,2048]{1,0:T(8,128)(2,1)} %get-tuple-element.5, bf16[512,2176]{1,0:T(8,128)(2,1)} %get-tuple-element.4), kind=kOutput, calls=%fused_computation.37 | convolution fusion | flops 538443264 | bytes 5769216 | tf_op jit(solution)/shard_map/dot_general | solution.py:15
  57.4 3.5 %fusion.103 = (f32[512]{0:T(512)S(1)}, f32[512,1024]{1,0:T(8,128)S(1)}) fusion(f32[512,1024]{1,0:T(8,128)S(1)} %get-tuple-element.40, bf16[1024,2048]{1,0:T(8,128)(2,1)} %get-tuple-element.5, bf16[512,2176]{1,0:T(8,128)(2,1)} %get-tuple-element.4), kind=kOutput, calls=%fused_computation.152 | convolution fusion | flops 1075314176 | bytes 7342080 | tf_op jit(solution)/shard_map/dot_general | solution.py:15
  63.5 9.0 %totals.1 = f32[16,512]{1,0:T(8,128)} custom-call(f32[16,512]{1,0:T(8,128)} %pad.4.lse_ref), custom_call_target="tpu_custom_call" | custom-call | tf_op jit(solution)/shard_map/totals/pallas_call | solution.py:365
  73.5 9.4 %fusion.17 = (bf16[512,1024]{1,0:T(8,128)(2,1)S(1)}, bf16[512,1024]{1,0:T(8,128)(2,1)S(1)}, bf16[512,1024]{1,0:T(8,128)(2,1)S(1)}, bf16[512,1024]{1,0:T(8,128)(2...) fusion(f32[512,1024]{1,0:T(8,128)S(1)} %get-tuple-element.26, ...), kind=kLoop, calls=%fused_computation.26 | loop fusion | flops 27787264 | bytes 27287552 | tf_op jit(solution)/shard_map/convert_element_type | solution.py:45
  83.5 2.2 %fusion.90 = f32[1024,8]{1,0:T(8,128)} fusion(bf16[512,1024]{1,0:T(8,128)(2,1)S(1)} %get-tuple-element.6, bf16[512,2176]{1,0:T(8,128)(2,1)} %get-tuple-element.4), kind=kOutput, calls=%fused_computation.126 | convolution fusion | flops 8388608 | bytes 1212416 | tf_op jit(solution)/shard_map/dot_general | solution.py:55
  86.8 2.2 %fusion.54 = f32[1024,8]{1,0:T(8,128)} fusion(bf16[512,1024]{1,0:T(8,128)(2,1)S(1)} %get-tuple-element.7, bf16[512,2176]{1,0:T(8,128)(2,1)} %get-tuple-element.4), kind=kOutput, calls=%fused_computation.86 | convolution fusion | flops 8388608 | bytes 1212416 | tf_op jit(solution)/shard_map/dot_general | solution.py:55
  90.3 2.2 %fusion.50 = f32[1024,16]{1,0:T(8,128)} fusion(bf16[512,1024]{1,0:T(8,128)(2,1)S(1)} %get-tuple-element.8, bf16[512,2176]{1,0:T(8,128)(2,1)} %get-tuple-element.4), kind=kOutput, calls=%fused_computation.82 | convolution fusion | flops 16777216 | bytes 1245184 | tf_op jit(solution)/shard_map/dot_general | solution.py:55
  93.8 2.3 %fusion.46 = f32[1024,32]{1,0:T(8,128)} fusion(bf16[512,1024]{1,0:T(8,128)(2,1)S(1)} %get-tuple-element.9, bf16[512,2176]{1,0:T(8,128)(2,1)} %get-tuple-element.4), kind=kOutput, calls=%fused_computation.78 | convolution fusion | flops 33554432 | bytes 1310720 | tf_op jit(solution)/shard_map/dot_general | solution.py:55
  97.3 2.2 %fusion.42 = f32[1024,64]{1,0:T(8,128)} fusion(bf16[512,1024]{1,0:T(8,128)(2,1)S(1)} %get-tuple-element.10, bf16[512,2176]{1,0:T(8,128)(2,1)} %get-tuple-element.4), kind=kOutput, calls=%fused_computation.74 | convolution fusion | flops 67108864 | bytes 1441792 | tf_op jit(solution)/shard_map/dot_general | solution.py:55
  100.7 2.2 %fusion.38 = f32[1024,128]{1,0:T(8,128)} fusion(bf16[512,1024]{1,0:T(8,128)(2,1)S(1)} %get-tuple-element.11, bf16[512,2176]{1,0:T(8,128)(2,1)} %get-tuple-element.4), kind=kOutput, calls=%fused_computation.70 | convolution fusion | flops 134217728 | bytes 1703936 | tf_op jit(solution)/shard_map/dot_general | solution.py:55
  104.1 2.4 %fusion.34 = f32[1024,256]{1,0:T(8,128)} fusion(bf16[512,1024]{1,0:T(8,128)(2,1)S(1)} %get-tuple-element.12, bf16[512,2176]{1,0:T(8,128)(2,1)} %get-tuple-element.4), kind=kOutput, calls=%fused_computation.66 | convolution fusion | flops 268435456 | bytes 2359296 | tf_op jit(solution)/shard_map/dot_general | solution.py:55
  109.6 5.9 %concatenate.14.pq_ref = f32[512,2048]{1,0:T(8,128)} concatenate(f32[512,8]{1,0:T(8,128)S(1)} %fusion.76, f32[512,8]{1,0:T(8,128)} %fusion.56, f32[512,16]{1,0:T(8,128)} %fusion.52, f32[512,32]{1,0:T(8,128)} %fusion.48, f32[512,64]{1,0:T(8,128)} %fusion.44, f32[512,128]{1,0:T(8,128)} %fusion.40, f32[512,256]{1,0:T(8,128)} %fusion.36, f32[512,512]{1,0:T(8,128)} %fusion.28, ...), dimensions={1} | concatenate | bytes 8388608 | tf_op jit(solution)/shard_map/concatenate | solution.py:65
  115.5 1.9 %fusion.31 = f32[1024,512]{1,0:T(8,128)S(1)} fusion(bf16[512,1024]{1,0:T(8,128)(2,1)S(1)} %get-tuple-element.13, bf16[512,2176]{1,0:T(8,128)(2,1)} %get-tuple-element.4), kind=kOutput, calls=%fused_computation.63 | convolution fusion | flops 536870912 | bytes 3670016 | tf_op jit(solution)/shard_map/dot_general | solution.py:55
  117.5 4.8 %fusion.25 = f32[1024,1024]{1,0:T(8,128)} fusion(bf16[512,2176]{1,0:T(8,128)(2,1)} %get-tuple-element.4, f32[512,1024]{1,0:T(8,128)S(1)} %copy-done.9, s32[1024]{0:T(1024)S(1)} %concatenate.13, f32[512]{0:T(512)S(1)} %bitcast.53, s32[512]{0:T(512)S(1)} %fusion.63), kind=kOutput, calls=%fused_computation.57 | convolution fusion | flops 1076887552 | bytes 7348224 | tf_op jit(solution)/shard_map/dot_general | solution.py:55
  122.3 9.9 %concatenate.15.pd_ref = f32[1024,2048]{1,0:T(8,128)} concatenate(f32[1024,8]{1,0:T(8,128)} %fusion.90, f32[1024,8]{1,0:T(8,128)} %fusion.54, f32[1024,16]{1,0:T(8,128)} %fusion.50, f32[1024,32]{1,0:T(8,128)} %fusion.46, f32[1024,64]{1,0:T(8,128)} %fusion.42, f32[1024,128]{1,0:T(8,128)} %fusion.38, f32[1024,256]{1,0:T(8,128)S(1)} %copy-done.11, f32[1024,512]{1,0:T(8,128)S(1)} %fusion.31, ...), dimensions={1} | concatenate | bytes 16777216 | tf_op jit(solution)/shard_map/concatenate | solution.py:65
  132.1 32.9 %reduce.3 = (f32[64,2048]{1,0:T(8,128)}, f32[64,2048]{1,0:T(8,128)}) custom-call(f32[512,2048]{1,0:T(8,128)} %concatenate.14.pq_ref, f32[1024,2048]{1,0:T(8,128)} %concatenate.15.pd_ref), custom_call_target="tpu_custom_call" | custom-call | tf_op jit(solution)/shard_map/reduce/pallas_call | solution.py:297
  165.1 1.9 %copy.58 = f32[64,2048]{1,0:T(8,128)} copy(f32[64,2048]{1,0:T(8,128)} %get-tuple-element.71) | data formatting | bytes 1048576
  167.0 1.9 %copy.59 = f32[64,2048]{1,0:T(8,128)} copy(f32[64,2048]{1,0:T(8,128)} %get-tuple-element.72) | data formatting | bytes 1048576
  (64 shorter events, 25.5 us)
Async XLA Ops:
  42.1 2.4 %copy-start = (f32[512,1024]{1,0:T(8,128)}, f32[512,1024]{1,0:T(8,128)S(1)}, u32[]{:S(2)}) copy-start(f32[512,1024]{1,0:T(8,128)S(1)} %get-tuple-element.28) | copy-start | bytes 6291460
  44.5 2.3 %copy-start.1 = (f32[512,1024]{1,0:T(8,128)}, f32[512,1024]{1,0:T(8,128)S(1)}, u32[]{:S(2)}) copy-start(f32[512,1024]{1,0:T(8,128)S(1)} %get-tuple-element.30) | copy-start | bytes 6291460
  46.9 2.4 %copy-start.2 = (f32[512,1024]{1,0:T(8,128)}, f32[512,1024]{1,0:T(8,128)S(1)}, u32[]{:S(2)}) copy-start(f32[512,1024]{1,0:T(8,128)S(1)} %get-tuple-element.32) | copy-start | bytes 6291460
  49.2 2.3 %copy-start.3 = (f32[512,1024]{1,0:T(8,128)}, f32[512,1024]{1,0:T(8,128)S(1)}, u32[]{:S(2)}) copy-start(f32[512,1024]{1,0:T(8,128)S(1)} %get-tuple-element.34) | copy-start | bytes 6291460
  51.5 2.4 %copy-start.4 = (f32[512,1024]{1,0:T(8,128)}, f32[512,1024]{1,0:T(8,128)S(1)}, u32[]{:S(2)}) copy-start(f32[512,1024]{1,0:T(8,128)S(1)} %get-tuple-element.36) | copy-start | bytes 6291460
  53.9 3.0 %copy-start.5 = (f32[512,1024]{1,0:T(8,128)}, f32[512,1024]{1,0:T(8,128)S(1)}, u32[]{:S(2)}) copy-start(f32[512,1024]{1,0:T(8,128)S(1)} %get-tuple-element.38) | copy-start | bytes 6291460
  56.9 4.0 %copy-start.6 = (f32[512,1024]{1,0:T(8,128)}, f32[512,1024]{1,0:T(8,128)S(1)}, u32[]{:S(2)}) copy-start(f32[512,1024]{1,0:T(8,128)S(1)} %get-tuple-element.40) | copy-start | bytes 6291460
  60.9 1.3 copy-start.7
  73.5 9.5 %copy-start.10 = (bf16[1024,2048]{1,0:T(8,128)(2,1)S(1)}, bf16[1024,2048]{1,0:T(8,128)(2,1)}, u32[]{:S(2)}) copy-start(bf16[1024,2048]{1,0:T(8,128)(2,1)} %get-tuple-element.5) | copy-start | bytes 12582916
  106.5 1.7 %copy-start.8 = (f32[512,1024]{1,0:T(8,128)S(1)}, f32[512,1024]{1,0:T(8,128)}, u32[]{:S(2)}) copy-start(f32[512,1024]{1,0:T(8,128)} %copy-done.7) | copy-start | bytes 6291460
  115.5 1.9 %copy-start.9 = (f32[512,1024]{1,0:T(8,128)S(1)}, f32[512,1024]{1,0:T(8,128)}, u32[]{:S(2)}) copy-start(f32[512,1024]{1,0:T(8,128)} %copy-done.7) | copy-start | bytes 6291460
  117.5 4.8 %copy-start.11 = (f32[1024,256]{1,0:T(8,128)S(1)}, f32[1024,256]{1,0:T(8,128)}, u32[]{:S(2)}) copy-start(f32[1024,256]{1,0:T(8,128)} %fusion.34) | copy-start | bytes 3145732

commit v3 on v2

--- a/solution.py
+++ b/solution.py
@@ -8,63 +8,8 @@
 from jax.sharding import PartitionSpec as P
 
 WIDTHS = 9
+LOG2_E = 1.4426950408889634
 logit_gain = 3.0
-
-
-def contract(first_op, second_op):
-    return lax.dot_general(
-        first_op, second_op, (((1,), (1,)), ((), ())), preferred_element_type=jnp.float32
-    )
-
-
-def width_list(feature_dim):
-    return [feature_dim >> WIDTHS - 1 - nested for nested in range(WIDTHS)]
-
-
-def scores(first_op, second_op):
-    uppers = width_list(first_op.shape[1])
-    result = []
-    running = jnp.zeros((first_op.shape[0], second_op.shape[0]), jnp.float32)
-    lower_col = 0
-    for upper_col in uppers:
-        running = running + contract(
-            first_op[:, lower_col:upper_col], second_op[:, lower_col:upper_col]
-        )
-        result.append(running * (logit_gain * upper_col ** (-0.5)))
-        lower_col = upper_col
-    return result
-
-
-def band_sums(logit_list, total_list, target, uppers):
-    bands = [None] * len(uppers)
-    running = None
-    for nested in reversed(range(len(uppers))):
-        scale = logit_gain * uppers[nested] ** (-0.5)
-        weight = (jnp.exp(logit_list[nested] - total_list[nested]) - target) * scale
-        running = weight if running is None else running + weight
-        bands[nested] = running.astype(jnp.bfloat16)
-    return bands
-
-
-def spread(bands, operand, uppers, transposed):
-    pieces = []
-    lower_col = 0
-    for nested, upper_col in enumerate(uppers):
-        block_part = operand[:, lower_col:upper_col]
-        if transposed:
-            product = lax.dot_general(
-                bands[nested],
-                block_part,
-                (((0,), (0,)), ((), ())),
-                preferred_element_type=jnp.float32,
-            )
-        else:
-            product = jnp.dot(bands[nested], block_part, preferred_element_type=jnp.float32)
-        pieces.append(product)
-        lower_col = upper_col
-    return jnp.concatenate(pieces, axis=1)
-
-
 AXES = ("y", "zl", "x", "core", "zh")
 MESH = pl.DeviceIdType.MESH
 VMEM = pl.BlockSpec(memory_space=pltpu.VMEM)
@@ -187,6 +132,223 @@
         compiler_params=pltpu.CompilerParams(collective_id=0, has_side_effects=True),
         name="gather",
     )(queries, documents)
+
+
+def contract(first_op, second_op, first_dim, second_dim):
+    return lax.dot_general(
+        first_op,
+        second_op,
+        (((first_dim,), (second_dim,)), ((), ())),
+        preferred_element_type=jnp.float32,
+    )
+
+
+def width_list(feature_dim):
+    return [feature_dim >> WIDTHS - 1 - nested for nested in range(WIDTHS)]
+
+
+def exchange_totals(lse, parts, total, sent, landed):
+    chips = lax.axis_size("y")
+    copies = []
+    for number, (step, pair, device) in enumerate(row_peers()):
+        back = (chips - step) % chips
+        copy = pltpu.make_async_remote_copy(
+            src_ref=lse,
+            dst_ref=parts.at[back * 2 + pair],
+            send_sem=sent.at[number],
+            recv_sem=landed.at[back * 2 + pair],
+            device_id=device,
+            device_id_type=MESH,
+        )
+        copy.start()
+        copies.append(copy)
+    for copy in copies:
+        copy.wait()
+    mine = lse[...]
+    group = mine.shape[1] // chips
+
+    def aligned(step, pair, place):
+        if step == 0 and pair == 0:
+            return mine[:, place * group : (place + 1) * group]
+        at = (place - step) % chips * group
+        piece = parts[step * 2 + pair, :, at : at + group]
+        return pltpu.roll(piece, group // 2, 1) if pair else piece
+
+    for place in range(chips):
+        pieces = [aligned(step, pair, place) for step in range(chips) for pair in range(2)]
+        peak = functools.reduce(jnp.maximum, pieces)
+        mass = sum(jnp.exp(piece - peak) for piece in pieces)
+        total[:, place * group : (place + 1) * group] = peak + jnp.log(mass)
+
+
+def row_peers():
+    chips = lax.axis_size("y")
+    y = lax.axis_index("y")
+    zl = lax.axis_index("zl")
+    return [
+        (step, pair, {"y": lax.rem(y + step, chips), "zl": lax.rem(zl + pair, 2)})
+        for step in range(chips)
+        for pair in range(2)
+        if step or pair
+    ]
+
+
+def first_id(place, own):
+    y, zl, x, core, zh = [lax.axis_index(axis) for axis in AXES]
+    chips = lax.axis_size("x")
+    step, pair, other = place // 4, lax.rem(place // 2, 2), lax.rem(place, 2)
+    chip = (y * 2 + lax.rem(zl + pair, 2)) * chips + lax.rem(x + step, chips)
+    return ((chip * 2 + lax.rem(core + other, 2)) * 2 + lax.rem(zh + pair, 2)) * own
+
+
+def middle_kernel(
+    rows_ref, docs_ref, pq_ref, pd_ref, logits, bands, peaks, lse, parts, total, partner, sent, landed
+):
+    count, dim = docs_ref.shape
+    width = rows_ref.shape[0]
+    own = count // 16
+    uppers = width_list(dim)
+    lowers = [0] + uppers[:-1]
+    scales = [logit_gain * upper ** (-0.5) for upper in uppers]
+    narrow = 256
+    few = uppers.index(narrow) + 1
+    meet([device for _, _, device in row_peers()])
+
+    marks = jnp.transpose(rows_ref[:, dim : dim + 128].astype(jnp.float32))
+    partner[...] = (marks[0:1] * 128.0 + marks[1:2]).astype(jnp.int32)
+
+    tall = count // 2
+
+    def score_block(block, carry):
+        at = pl.ds(pl.multiple_of(block * tall, tall), tall)
+        lane = lax.broadcasted_iota(jnp.int32, (tall, narrow), 1)
+        head = docs_ref[at, :narrow]
+        for nested in range(few):
+            cut = jnp.where(lane < uppers[nested], head, jnp.zeros_like(head))
+            logits[nested, at, :] = contract(cut, rows_ref[:, :narrow], 1, 1)
+        for nested in range(few, WIDTHS):
+            cols = slice(lowers[nested], uppers[nested])
+            logits[nested, at, :] = logits[nested - 1, at, :] + contract(
+                docs_ref[at, cols], rows_ref[:, cols], 1, 1
+            )
+        return carry
+
+    lax.fori_loop(0, 2, score_block, 0)
+
+    lse[...] = jnp.zeros_like(lse)
+    step_rows = 64
+    for nested in range(WIDTHS):
+
+        def peak_block(block, best):
+            at = pl.ds(pl.multiple_of(block * step_rows, step_rows), step_rows)
+            piece = logits[nested, at, :].reshape(step_rows // 8, 8, width)
+            return jnp.maximum(best, jnp.max(piece, axis=0))
+
+        best = lax.fori_loop(
+            0, count // step_rows, peak_block, jnp.full((8, width), -jnp.inf, jnp.float32)
+        )
+        peak = jnp.max(best, axis=0, keepdims=True)
+
+        def mass_block(block, mass):
+            at = pl.ds(pl.multiple_of(block * step_rows, step_rows), step_rows)
+            piece = jnp.exp2((logits[nested, at, :] - peak) * (scales[nested] * LOG2_E))
+            logits[nested, at, :] = piece
+            return mass + jnp.sum(piece.reshape(step_rows // 8, 8, width), axis=0)
+
+        mass = lax.fori_loop(0, count // step_rows, mass_block, jnp.zeros((8, width), jnp.float32))
+        mass = jnp.sum(mass, axis=0, keepdims=True)
+        peaks[nested : nested + 1, :] = peak * scales[nested]
+        lse[nested : nested + 1, :] = peak * scales[nested] + jnp.log(mass)
+
+    exchange_totals(lse, parts, total, sent, landed)
+
+    for nested in range(WIDTHS):
+        row = slice(nested, nested + 1)
+        peaks[row, :] = jnp.exp(peaks[row, :] - total[row, :]) * scales[nested]
+    short = 32
+
+    def band_block(block, carry):
+        at = pl.ds(pl.multiple_of(block * short, short), short)
+        per = own // short
+        base = first_id(block // per, own) + lax.rem(block, per) * short
+        ids = base + lax.broadcasted_iota(jnp.int32, (short, width), 0)
+        hit = ids == partner[...]
+        running = jnp.zeros((short, width), jnp.float32)
+        gone = 0.0
+        for nested in reversed(range(WIDTHS)):
+            running = running + logits[nested, at, :] * peaks[nested : nested + 1, :]
+            gone += scales[nested]
+            band = running - jnp.where(hit, gone, 0.0)
+            bands[at, nested * width : (nested + 1) * width] = band.astype(jnp.bfloat16)
+        return carry
+
+    lax.fori_loop(0, count // short, band_block, 0)
+
+    piece = 256
+
+    def doc_block(block, carry):
+        at = pl.ds(pl.multiple_of(block * piece, piece), piece)
+        lane = lax.broadcasted_iota(jnp.int32, (piece, narrow), 1)
+        head = None
+        for nested in range(WIDTHS):
+            cols = slice(0, narrow) if nested < few else slice(lowers[nested], uppers[nested])
+            part = contract(
+                bands[at, nested * width : (nested + 1) * width], rows_ref[:, cols], 1, 0
+            )
+            if nested < few:
+                head = part if head is None else jnp.where(lane < lowers[nested], head, part)
+                part = head
+            if nested >= few - 1:
+                pd_ref[at, cols] = part
+        return carry
+
+    lax.fori_loop(0, count // piece, doc_block, 0)
+
+    def row_block(block, carry):
+        at = pl.ds(pl.multiple_of(block * piece, piece), piece)
+        lane = lax.broadcasted_iota(jnp.int32, (piece, narrow), 1)
+        head = None
+        for nested in range(WIDTHS):
+            cols = slice(0, narrow) if nested < few else slice(lowers[nested], uppers[nested])
+            start = pl.multiple_of(nested * width + block * piece, piece)
+            part = contract(bands[:, pl.ds(start, piece)], docs_ref[:, cols], 0, 0)
+            if nested < few:
+                head = part if head is None else jnp.where(lane < lowers[nested], head, part)
+                part = head
+            if nested >= few - 1:
+                pq_ref[at, cols] = part
+        return carry
+
+    lax.fori_loop(0, width // piece, row_block, 0)
+
+
+def middle(rows, docs):
+    count, dim = docs.shape
+    width = rows.shape[0]
+    return pl.pallas_call(
+        middle_kernel,
+        out_shape=(
+            jax.ShapeDtypeStruct((width, dim), jnp.float32),
+            jax.ShapeDtypeStruct((count, dim), jnp.float32),
+        ),
+        in_specs=[VMEM] * 2,
+        out_specs=(VMEM, VMEM),
+        scratch_shapes=[
+            pltpu.VMEM((WIDTHS, count, width), jnp.float32),
+            pltpu.VMEM((count, WIDTHS * width), jnp.bfloat16),
+            pltpu.VMEM((16, width), jnp.float32),
+            pltpu.VMEM((16, width), jnp.float32),
+            pltpu.VMEM((8, 16, width), jnp.float32),
+            pltpu.VMEM((16, width), jnp.float32),
+            pltpu.VMEM((1, width), jnp.int32),
+            pltpu.SemaphoreType.DMA((8,)),
+            pltpu.SemaphoreType.DMA((8,)),
+        ],
+        compiler_params=pltpu.CompilerParams(
+            collective_id=2, has_side_effects=True, vmem_limit_bytes=60 * 2**20
+        ),
+        name="middle",
+    )(rows, docs)
 
 
 def reduce_kernel(pq_ref, pd_ref, gq_ref, gd_ref, sib, far_s, near_s, far_r, near_r, pair_s, pair_r, sent, landed):
@@ -317,110 +479,14 @@
     )(part_queries, part_documents)
 
 
-def totals_kernel(lse_ref, out_ref, parts, sent, landed):
-    chips = lax.axis_size("y")
-    y = lax.axis_index("y")
-    zl = lax.axis_index("zl")
-    peers = []
-    for step in range(chips):
-        for pair in range(2):
-            if step or pair:
-                peers.append(
-                    (step, pair, {"y": lax.rem(y + step, chips), "zl": lax.rem(zl + pair, 2)})
-                )
-    meet([device for _, _, device in peers])
-    copies = []
-    for number, (step, pair, device) in enumerate(peers):
-        back = (chips - step) % chips
-        copy = pltpu.make_async_remote_copy(
-            src_ref=lse_ref,
-            dst_ref=parts.at[back * 2 + pair],
-            send_sem=sent.at[number],
-            recv_sem=landed.at[back * 2 + pair],
-            device_id=device,
-            device_id_type=MESH,
-        )
-        copy.start()
-        copies.append(copy)
-    mine = lse_ref[...]
-    for copy in copies:
-        copy.wait()
-    group = mine.shape[1] // chips
-
-    def aligned(step, pair, place):
-        if step == 0 and pair == 0:
-            return mine[:, place * group : (place + 1) * group]
-        at = (place - step) % chips * group
-        piece = parts[step * 2 + pair, :, at : at + group]
-        return pltpu.roll(piece, group // 2, 1) if pair else piece
-
-    for place in range(chips):
-        pieces = [aligned(step, pair, place) for step in range(chips) for pair in range(2)]
-        peak = functools.reduce(jnp.maximum, pieces)
-        mass = sum(jnp.exp(piece - peak) for piece in pieces)
-        out_ref[:, place * group : (place + 1) * group] = peak + jnp.log(mass)
-
-
-def combined_totals(lse):
-    return pl.pallas_call(
-        totals_kernel,
-        out_shape=jax.ShapeDtypeStruct(lse.shape, jnp.float32),
-        in_specs=[VMEM],
-        out_specs=VMEM,
-        scratch_shapes=[
-            pltpu.VMEM((8, *lse.shape), jnp.float32),
-            pltpu.SemaphoreType.DMA((8,)),
-            pltpu.SemaphoreType.DMA((8,)),
-        ],
-        compiler_params=pltpu.CompilerParams(collective_id=2, has_side_effects=True),
-        name="totals",
-    )(lse)
-
-
-def row_ids(own):
-    y, zl, x, core, zh = [lax.axis_index(axis) for axis in AXES]
-    chips = lax.axis_size("x")
-    ids = []
-    for step in range(chips):
-        for pair in range(2):
-            for other in range(2):
-                there_x = lax.rem(x + step, chips)
-                there_zl = lax.rem(zl + pair, 2)
-                there_zh = lax.rem(zh + pair, 2)
-                there_core = lax.rem(core + other, 2)
-                chip = (y * 2 + there_zl) * chips + there_x
-                shard = (chip * 2 + there_core) * 2 + there_zh
-                ids.append(shard * own + jnp.arange(own, dtype=jnp.int32))
-    return jnp.concatenate(ids)
-
-
 def on_device(queries, documents, partner):
-    own, dim = queries.shape
-    uppers = width_list(dim)
     index = partner.astype(jnp.float32)
     high = jnp.floor(index / 128.0)
     low = index - 128.0 * high
     lane = jnp.arange(128)[None]
     extra = jnp.where(lane == 0, high[:, None], jnp.where(lane == 1, low[:, None], 0.0))
     rows, docs = gather(jnp.concatenate([queries, extra.astype(jnp.bfloat16)], axis=1), documents)
-    marks = rows[:, dim : dim + 2].astype(jnp.float32)
-    row_partner = (marks[:, 0] * 128.0 + marks[:, 1]).astype(jnp.int32)
-    rows = rows[:, :dim]
-    target = (row_partner[:, None] == row_ids(own)[None, :]).astype(jnp.float32)
-    logit_list = scores(rows, docs)
-    row_peaks = jnp.stack([jnp.max(logits, axis=1) for logits in logit_list])
-    masses = jnp.stack(
-        [
-            jnp.sum(jnp.exp(logits - row_peaks[nested][:, None]), axis=1)
-            for nested, logits in enumerate(logit_list)
-        ]
-    )
-    lse = jnp.pad(row_peaks + jnp.log(masses), ((0, 16 - WIDTHS), (0, 0)))
-    totals = combined_totals(lse)
-    bands = band_sums(
-        logit_list, [totals[nested][:, None] for nested in range(len(uppers))], target, uppers
-    )
-    return reduce(spread(bands, docs, uppers, False), spread(bands, rows, uppers, True))
+    return reduce(*middle(rows, docs))
 
 
 def solution(mesh):

time: 170 us -> 110 us (0.65)
  matrix products: 51.5 us -> 0 us
  Pallas kernels: 76 us -> 103 us
  local copies, waits for them, and re-layouts: 22.7 us -> 3.74 us
  other arithmetic: 17.7 us -> 2.43 us
    dot_general x27 -> x0, matrix products: 51.5 us -> none  [the longest x9 22.4 us: spread(): lax.dot_general(bands[nested], block_part, (((0,), (0,)), ((), ())), pref...]
    pallas_call x1, Pallas kernels: 9.04 us -> 35.6 us  [middle(): pl.pallas_call(middle_kernel, out_shape=(jax.ShapeDtypeStruct((width, dim...]
    concatenate x3 -> x0, local copies, waits for them, and re-layouts: 15.9 us -> none  [the longest x2 15.8 us: spread(): return jnp.concatenate(pieces, axis=1)]
    convert_element_type x3 -> x0, other arithmetic: 10.6 us -> none  [the longest x1 9.44 us: band_sums(): bands[nested] = running.astype(jnp.bfloat16)]
    reduce_sum x9 -> x0, other arithmetic: 4.67 us -> none  [on_device(): jnp.sum(jnp.exp(logits - row_peaks[nested][:, None]), axis=1)]
    unnamed x26 -> x2, local copies, waits for them, and re-layouts: 5.09 us -> 3.74 us
where the time goes in v3:
time: 110 us
  Pallas kernels  103 us (94%)
  local copies, waits for them, and re-layouts  3.74 us (3%)
  other arithmetic  2.43 us (2%)
    pallas_call x1, Pallas kernels, middle(): pl.pallas_call(middle_kernel, out_shape=(jax.ShapeDtypeStruct((width, dim...  35.6 us
    pallas_call x1, Pallas kernels, gather(): pl.pallas_call(gather_kernel, out_shape=(jax.ShapeDtypeStruct((8 * own, w...  34 us
    pallas_call x1, Pallas kernels, reduce(): pl.pallas_call(reduce_kernel, out_shape=(piece, piece), in_specs=[VMEM] *...  33.1 us
    unnamed x2, local copies, waits for them, and re-layouts  3.74 us

profile of v3, /device:TPU:1, one launch (start us, length us, event | category | flops | bytes accessed | tf_op | source)
XLA Modules:
  0.0 109.5 jit_solution(1499955561902501927)
XLA Ops:
  0.6 0.7 multiply_floor_fusion
  1.3 0.1 select_convert_fusion
  1.4 1.7 %pad_maximum_fusion.q_ref = bf16[64,2176]{1,0:T(8,128)(2,1)} fusion(bf16[64,128]{1,0:T(8,128)(2,1)S(1)} %select_convert_fusion, bf16[64,2048]{1,0:T(8,128)(2,1)} %param.3), kind=kLoop, calls=%fused_computation | loop fusion | flops 557056 | bytes 557056 | tf_op jit(solution)/shard_map/concatenate | solution.py:488
  3.1 34.0 %gather.1 = (bf16[512,2176]{1,0:T(8,128)(2,1)}, bf16[1024,2048]{1,0:T(8,128)(2,1)}) custom-call(bf16[64,2176]{1,0:T(8,128)(2,1)} %pad_maximum_fusion.q_ref, bf16[64,2048]{1,0:T(8,128)(2,1)} %d_ref.1), custom_call_target="tpu_custom_call" | custom-call | tf_op jit(solution)/shard_map/gather/pallas_call | solution.py:123
  37.0 35.6 %middle.1 = (f32[512,2048]{1,0:T(8,128)}, f32[1024,2048]{1,0:T(8,128)}) custom-call(bf16[512,2176]{1,0:T(8,128)(2,1)} %get-tuple-element.6.rows_ref, bf16[1024,2048]{1,0:T(8,128)(2,1)} %get-tuple-element.7.docs_ref), custom_call_target="tpu_custom_call" | custom-call | tf_op jit(solution)/shard_map/middle/pallas_call | solution.py:328
  72.6 33.1 %reduce.1 = (f32[64,2048]{1,0:T(8,128)}, f32[64,2048]{1,0:T(8,128)}) custom-call(f32[512,2048]{1,0:T(8,128)} %get-tuple-element.8.pq_ref, f32[1024,2048]{1,0:T(8,128)} %get-tuple-element.9.pd_ref), custom_call_target="tpu_custom_call" | custom-call | tf_op jit(solution)/shard_map/reduce/pallas_call | solution.py:459
  105.8 1.9 %copy.7 = f32[64,2048]{1,0:T(8,128)} copy(f32[64,2048]{1,0:T(8,128)} %get-tuple-element.16) | data formatting | bytes 1048576
  107.6 1.9 %copy.8 = f32[64,2048]{1,0:T(8,128)} copy(f32[64,2048]{1,0:T(8,128)} %get-tuple-element.17) | data formatting | bytes 1048576
  (1 shorter events, 0.0 us)

commit v4 on v1

v4 whole, which is shorter than its diff:
```python
import functools
import jax
import jax.numpy as jnp
from jax import lax
from jax.experimental import pallas as pl
from jax.experimental.pallas import tpu as pltpu
from jax.sharding import Mesh
from jax.sharding import PartitionSpec as P

WIDTHS = 9
LOG2_E = 1.4426950408889634
logit_gain = 3.0

AXES = ("y", "zl", "x", "core", "zh")
MESH = pl.DeviceIdType.MESH
VMEM = pl.BlockSpec(memory_space=pltpu.VMEM)


def width_list(feature_dim):
    return [feature_dim >> WIDTHS - 1 - nested for nested in range(WIDTHS)]


def contract(first_op, second_op, first_dim, second_dim):
    return lax.dot_general(
        first_op,
        second_op,
        (((first_dim,), (second_dim,)), ((), ())),
        preferred_element_type=jnp.float32,
    )


def neighbours(axis):
    size = lax.axis_size(axis)
    me = lax.axis_index(axis)
    up = {axis: lax.rem(me + 1, size)}
    down = {axis: lax.rem(me + size - 1, size)}
    pair = {"zl": 1 - lax.axis_index("zl")}
    if axis == "x":
        pair["zh"] = 1 - lax.axis_index("zh")
    return up, down, pair


def row_peers():
    chips = lax.axis_size("y")
    y = lax.axis_index("y")
    zl = lax.axis_index("zl")
    return [
        (step, pair, {"y": lax.rem(y + step, chips), "zl": lax.rem(zl + pair, 2)})
        for step in range(chips)
        for pair in range(2)
        if step or pair
    ]


def first_id(place, own):
    y, zl, x, core, zh = [lax.axis_index(axis) for axis in AXES]
    chips = lax.axis_size("x")
    step, pair, other = place // 4, lax.rem(place // 2, 2), lax.rem(place, 2)
    chip = (y * 2 + lax.rem(zl + pair, 2)) * chips + lax.rem(x + step, chips)
    return ((chip * 2 + lax.rem(core + other, 2)) * 2 + lax.rem(zh + pair, 2)) * own


def meet(devices):
    barrier = pltpu.get_barrier_semaphore()
    for device in devices:
        pl.semaphore_signal(barrier, inc=1, device_id=device, device_id_type=MESH)
    pl.semaphore_wait(barrier, len(devices))


class Sender:
    def __init__(self, sent, landed):
        self.sent, self.landed, self.started = sent, landed, []

    def __call__(self, src, dst, device, number=None, arrival=None):
        number = len(self.started)
        copy = pltpu.make_async_remote_copy(
            src_ref=src,
            dst_ref=dst,
            send_sem=self.sent.at[number],
            recv_sem=self.landed.at[number if arrival is None else arrival],
            device_id=device,
            device_id_type=MESH,
        )
        copy.start()
        self.started.append(copy)
        return copy

    def finish(self):
        for copy in self.started:
            copy.wait_send()


def gather(send, q_ref, d_ref, rows_ref, docs_ref):
    own = q_ref.shape[0]
    half = own // 2
    sibling = {"core": 1 - lax.axis_index("core")}

    def q_slot(step, pair, lo=0, count=own):
        return rows_ref.at[pl.ds((step * 2 + pair) * own + lo, count), :]

    def d_slot(step, pair, other=0, lo=0, count=own):
        return docs_ref.at[pl.ds(((step * 2 + pair) * 2 + other) * own + lo, count), :]

    lanes = ((q_ref, q_slot, *neighbours("y")), (d_ref, d_slot, *neighbours("x")))
    first = []
    for src, slot, up, down, pair in lanes:
        first.append(
            (
                send(src, slot(0, 1), pair),
                send(src, slot(3, 0), up),
                send(src, slot(1, 0), down),
            )
        )
    across = [send(d_ref, d_slot(0, 0, 1), sibling)]
    rows_ref[pl.ds(0, own), :] = q_ref[...]
    docs_ref[pl.ds(0, own), :] = d_ref[...]
    second = []
    for (src, slot, up, down, pair), copies in zip(lanes, first):
        copies[0].wait_recv()
        second.append(
            (
                send(slot(0, 1), slot(3, 1), up),
                send(slot(0, 1), slot(1, 1), down),
            )
        )
    across.append(send(d_slot(0, 1), d_slot(0, 1, 1), sibling))
    far = []
    for pair, stage in ((0, first), (1, second)):
        for (src, slot, up, down, _), copies in zip(lanes, stage):
            for copy, step, device, lo in ((copies[-2], 3, up, 0), (copies[-1], 1, down, half)):
                copy.wait_recv()
                far.append(
                    send(
                        slot(step, pair, lo=lo, count=half),
                        slot(2, pair, lo=lo, count=half),
                        device,
                    )
                )
        for step in (3, 1):
            across.append(send(d_slot(step, pair), d_slot(step, pair, 1), sibling))
    for copy in far:
        copy.wait_recv()
    for pair in range(2):
        across.append(send(d_slot(2, pair), d_slot(2, pair, 1), sibling))
    for copy in across:
        copy.wait_recv()


def exchange_totals(send, lse, parts, total):
    chips = lax.axis_size("y")
    copies = [
        send(lse, parts.at[(chips - step) % chips * 2 + pair], device)
        for step, pair, device in row_peers()
    ]
    for copy in copies:
        copy.wait_recv()
    mine = lse[...]
    group = mine.shape[1] // chips

    def aligned(step, pair, place):
        if step == 0 and pair == 0:
            return mine[:, place * group : (place + 1) * group]
        at = (place - step) % chips * group
        piece = parts[step * 2 + pair, :, at : at + group]
        return pltpu.roll(piece, group // 2, 1) if pair else piece

    for place in range(chips):
        pieces = [aligned(step, pair, place) for step in range(chips) for pair in range(2)]
        peak = functools.reduce(jnp.maximum, pieces)
        mass = sum(jnp.exp(piece - peak) for piece in pieces)
        total[:, place * group : (place + 1) * group] = peak + jnp.log(mass)


def step_kernel(
    q_ref,
    d_ref,
    p_ref,
    gq_ref,
    gd_ref,
    rows_ref,
    docs_ref,
    logits,
    bands,
    peaks,
    lse,
    parts,
    total,
    marks,
    pq_ref,
    pd_ref,
    sib,
    far_s,
    near_s,
    far_r,
    near_r,
    pair_s,
    pair_r,
    sent,
    landed,
):
    count, dim = docs_ref.shape
    width = rows_ref.shape[0]
    own = q_ref.shape[0]
    half = own // 2
    uppers = width_list(dim)
    lowers = [0] + uppers[:-1]
    scales = [logit_gain * upper ** (-0.5) for upper in uppers]
    narrow = 256
    few = uppers.index(narrow) + 1
    chips = lax.axis_size("y")
    sibling = {"core": 1 - lax.axis_index("core")}
    meet([device for _, _, device in row_peers()] + [*neighbours("x"), sibling])
    send = Sender(sent, landed)

    marked = [
        send(p_ref, marks.at[(chips - step) % chips * 2 + pair], device)
        for step, pair, device in row_peers()
    ]
    gather(send, q_ref, d_ref, rows_ref, docs_ref)

    tall = count // 2

    def score_block(block, carry):
        at = pl.ds(pl.multiple_of(block * tall, tall), tall)
        lane = lax.broadcasted_iota(jnp.int32, (tall, narrow), 1)
        head = docs_ref[at, :narrow]
        for nested in range(few):
            cut = jnp.where(lane < uppers[nested], head, jnp.zeros_like(head))
            logits[nested, at, :] = contract(cut, rows_ref[:, :narrow], 1, 1)
        for nested in range(few, WIDTHS):
            cols = slice(lowers[nested], uppers[nested])
            logits[nested, at, :] = logits[nested - 1, at, :] + contract(
                docs_ref[at, cols], rows_ref[:, cols], 1, 1
            )
        return carry

    lax.fori_loop(0, 2, score_block, 0)

    lse[...] = jnp.zeros_like(lse)
    step_rows = 64
    for nested in range(WIDTHS):

        def peak_block(block, best):
            at = pl.ds(pl.multiple_of(block * step_rows, step_rows), step_rows)
            piece = logits[nested, at, :].reshape(step_rows // 8, 8, width)
            return jnp.maximum(best, jnp.max(piece, axis=0))

        best = lax.fori_loop(
            0, count // step_rows, peak_block, jnp.full((8, width), -jnp.inf, jnp.float32)
        )
        peak = jnp.max(best, axis=0, keepdims=True)

        def mass_block(block, mass):
            at = pl.ds(pl.multiple_of(block * step_rows, step_rows), step_rows)
            piece = jnp.exp2((logits[nested, at, :] - peak) * (scales[nested] * LOG2_E))
            logits[nested, at, :] = piece
            return mass + jnp.sum(piece.reshape(step_rows // 8, 8, width), axis=0)

        mass = lax.fori_loop(0, count // step_rows, mass_block, jnp.zeros((8, width), jnp.float32))
        mass = jnp.sum(mass, axis=0, keepdims=True)
        peaks[nested : nested + 1, :] = peak * scales[nested]
        lse[nested : nested + 1, :] = peak * scales[nested] + jnp.log(mass)

    exchange_totals(send, lse, parts, total)
    for copy in marked:
        copy.wait_recv()

    for nested in range(WIDTHS):
        row = slice(nested, nested + 1)
        peaks[row, :] = jnp.exp(peaks[row, :] - total[row, :]) * scales[nested]
    side = lax.broadcasted_iota(jnp.int32, (1, 2 * own), 1)
    partner = []
    for step in range(chips):
        near_mark = p_ref[0:1, :] if step == 0 else marks[step * 2, 0:1, :]
        partner.append(jnp.where(side < own, near_mark, marks[step * 2 + 1, 0:1, :]))
    partner = jnp.concatenate(partner, axis=1)
    short = 32

    def band_block(block, carry):
        at = pl.ds(pl.multiple_of(block * short, short), short)
        per = own // short
        base = first_id(block // per, own) + lax.rem(block, per) * short
        ids = base + lax.broadcasted_iota(jnp.int32, (short, width), 0)
        hit = ids == partner
        running = jnp.zeros((short, width), jnp.float32)
        gone = 0.0
        for nested in reversed(range(WIDTHS)):
            running = running + logits[nested, at, :] * peaks[nested : nested + 1, :]
            gone += scales[nested]
            band = running - jnp.where(hit, gone, 0.0)
            bands[at, nested * width : (nested + 1) * width] = band.astype(jnp.bfloat16)
        return carry

    lax.fori_loop(0, count // short, band_block, 0)

    def bounds(nested):
        return slice(0, narrow) if nested < few else slice(lowers[nested], uppers[nested])

    def product(tall_rows, get, out_ref, at):
        lane = lax.broadcasted_iota(jnp.int32, (tall_rows, narrow), 1)
        head = None
        for nested in range(WIDTHS):
            part = get(nested, bounds(nested))
            if nested < few:
                head = part if head is None else jnp.where(lane < lowers[nested], head, part)
                part = head
            if nested >= few - 1:
                out_ref[at, bounds(nested)] = part

    across = {}

    def documents_for(step):
        piece = 4 * own
        at = slice(step * piece, (step + 1) * piece)
        product(
            piece,
            lambda nested, cols: contract(
                bands[at, nested * width : (nested + 1) * width], rows_ref[:, cols], 1, 0
            ),
            pd_ref,
            at,
        )
        for pair in (1, 0):
            theirs = pd_ref.at[pl.ds(((step * 2 + pair) * 2 + 1) * own, own), :]
            across[step, pair] = send(theirs, sib.at[step * 2 + pair], sibling)

    def queries_for(step):
        piece = 2 * own
        product(
            piece,
            lambda nested, cols: contract(
                bands[:, nested * width + step * piece : nested * width + (step + 1) * piece],
                docs_ref[:, cols],
                0,
                0,
            ),
            pq_ref,
            slice(step * piece, (step + 1) * piece),
        )

    def q_part(step, pair, lo=0, size=own):
        return pq_ref[pl.ds((step * 2 + pair) * own + lo, size), :]

    def d_part(step, pair, lo=0, size=own):
        mine = pd_ref[pl.ds((step * 2 + pair) * 2 * own + lo, size), :]
        return mine + sib[step * 2 + pair, pl.ds(lo, size), :]

    lanes = ((q_part, *neighbours("y")), (d_part, *neighbours("x")))
    far = {}
    near = {}

    def send_far(which, pair):
        part, up, down, _ = lanes[which]
        far_s[which, pair] = part(2, pair).astype(jnp.bfloat16)
        for way, device in ((0, up), (1, down)):
            piece = pl.ds(way * half, half)
            far[which, pair, way] = send(
                far_s.at[which, pair, piece], far_r.at[which, pair, piece], device
            )

    def send_near(which, pair):
        part, up, down, _ = lanes[which]
        for way, device, step in ((0, up, 1), (1, down, 3)):
            if which == 1:
                across[step, pair].wait_recv()
            far[which, pair, way].wait_recv()
            lo = way * half
            more = half - lo
            near_s[which, pair, way, pl.ds(lo, half), :] = (
                part(step, pair, lo, half)
                + far_r[which, pair, pl.ds(lo, half), :].astype(jnp.float32)
            ).astype(jnp.bfloat16)
            near_s[which, pair, way, pl.ds(more, half), :] = part(step, pair, more, half).astype(
                jnp.bfloat16
            )
            near[which, pair, way] = send(
                near_s.at[which, pair, way], near_r.at[which, pair, way], device
            )

    def arrived(which, pair):
        part = lanes[which][0]
        if which == 1:
            across[0, pair].wait_recv()
        near[which, pair, 0].wait_recv()
        near[which, pair, 1].wait_recv()
        return (
            part(0, pair)
            + near_r[which, pair, 0].astype(jnp.float32)
            + near_r[which, pair, 1].astype(jnp.float32)
        )

    documents_for(2)
    queries_for(2)
    send_far(0, 1)
    send_far(0, 0)
    for pair in (1, 0):
        across[2, pair].wait_recv()
        send_far(1, pair)
    documents_for(1)
    documents_for(3)
    queries_for(1)
    queries_for(3)
    for pair in (1, 0):
        send_near(0, pair)
        send_near(1, pair)
    documents_for(0)
    queries_for(0)
    last = []
    for which in range(2):
        pair_s[which] = arrived(which, 1).astype(jnp.bfloat16)
        last.append(send(pair_s.at[which], pair_r.at[which], lanes[which][3]))
    outs = (gq_ref, gd_ref)
    for which in range(2):
        outs[which][...] = arrived(which, 0)
    for which in range(2):
        last[which].wait_recv()
        outs[which][...] = outs[which][...] + pair_r[which].astype(jnp.float32)
    send.finish()


def on_device(queries, documents, partner):
    own, dim = queries.shape
    width, count = 8 * own, 16 * own
    piece = jax.ShapeDtypeStruct((own, dim), jnp.float32)
    wire = jnp.bfloat16
    copies = 7 + 26 + 7 + 30
    return pl.pallas_call(
        step_kernel,
        out_shape=(piece, piece),
        in_specs=[VMEM] * 3,
        out_specs=(VMEM, VMEM),
        scratch_shapes=[
            pltpu.VMEM((width, dim), wire),
            pltpu.VMEM((count, dim), wire),
            pltpu.VMEM((WIDTHS, count, width), jnp.float32),
            pltpu.VMEM((count, WIDTHS * width), wire),
            pltpu.VMEM((16, width), jnp.float32),
            pltpu.VMEM((16, width), jnp.float32),
            pltpu.VMEM((8, 16, width), jnp.float32),
            pltpu.VMEM((16, width), jnp.float32),
            pltpu.VMEM((8, 8, 2 * own), jnp.int32),
            pltpu.VMEM((width, dim), jnp.float32),
            pltpu.VMEM((count, dim), jnp.float32),
            pltpu.VMEM((8, own, dim), jnp.float32),
            pltpu.VMEM((2, 2, own, dim), wire),
            pltpu.VMEM((2, 2, 2, own, dim), wire),
            pltpu.VMEM((2, 2, own, dim), wire),
            pltpu.VMEM((2, 2, 2, own, dim), wire),
            pltpu.VMEM((2, own, dim), wire),
            pltpu.VMEM((2, own, dim), wire),
            pltpu.SemaphoreType.DMA((copies,)),
            pltpu.SemaphoreType.DMA((copies,)),
        ],
        compiler_params=pltpu.CompilerParams(
            collective_id=0, has_side_effects=True, vmem_limit_bytes=67043328
        ),
        name="step",
    )(queries, documents, jnp.tile(partner[None, :], (8, 2)))


def solution(mesh):
    finer = Mesh(mesh.devices.reshape(4, 2, 4, 2, mesh.shape["rep"]), AXES)
    placed = (P(AXES, None), P(AXES, None), P(AXES))
    return jax.shard_map(
        on_device,
        mesh=finer,
        in_specs=placed,
        out_specs=(P(AXES, None), P(AXES, None)),
        check_vma=False,
    )
```

time: 407 us -> 79.1 us (0.19)
  waiting for transfers between devices: 279 us -> 0 us
  Pallas kernels: 0 us -> 73.4 us
  matrix products: 45.7 us -> 0 us
  blocking collectives: 32.3 us -> 0 us
  local copies, waits for them, and re-layouts: 18.7 us -> 4.06 us
  other arithmetic: 14.4 us -> 0 us
  between operations: 14.7 us -> 0.65 us
    unnamed x5 -> x0, waiting for transfers between devices: 108 us -> none
    all_gather x2 -> x0, waiting for transfers between devices: 102 us -> none  [the longest x1 61.3 us: on_device(): docs = lax.all_gather(documents, D_AXES, axis=0, tiled=True)]
    pallas_call x0 -> x1, Pallas kernels: none -> 73.4 us  [on_device(): pl.pallas_call(step_kernel, out_shape=(piece, piece), in_specs=[VMEM] * 3...]
    reduce_scatter x1 -> x0, waiting for transfers between devices: 68.8 us -> none  [on_device(): lax.psum_scatter(spread(bands, docs, uppers, False), Q_AXES, scatter_dime...]
    dot_general x27 -> x0, matrix products: 45.7 us -> none  [the longest x9 18.1 us: contract(): lax.dot_general(first_op, second_op, (((1,), (1,)), ((), ())), preferred_...]
    all_gather x1 -> x0, blocking collectives: 22.3 us -> none  [on_device(): parts = lax.all_gather(row_peaks + jnp.log(masses), Q_AXES, axis=0)]
    unnamed x1 -> x0, blocking collectives: 10 us -> none
    unnamed x54 -> x4, local copies, waits for them, and re-layouts: 12.7 us -> 2.73 us
  transfers between devices with their start and end apart: 4 -> 0, of which waited for: 4 -> 0; matrix products, arithmetic and copies ran while one was open for 7% -> 0% of each run, Pallas kernels for 0% -> 0%
where the time goes in v4:
time: 79.1 us; the launch traced here: 78.1 us
  Pallas kernels  73.4 us (93%)
  local copies, waits for them, and re-layouts  4.06 us (5%)
    pallas_call x1, Pallas kernels, on_device(): pl.pallas_call(step_kernel, out_shape=(piece, piece), in_specs=[VMEM] * 3...  73.4 us
    unnamed x4, local copies, waits for them, and re-layouts  2.73 us

profile of v4, /device:TPU:1, one launch (start us, length us, event | category | flops | bytes accessed | tf_op | source)
XLA Modules:
  0.0 78.1 jit_solution(1404974615611586517)
XLA Ops:
  0.6 0.7 tile.10
  1.3 0.1 tile.11
  1.4 0.6 tile.12.p_ref
  2.0 73.4 %step.1 = (f32[64,2048]{1,0:T(8,128)}, f32[64,2048]{1,0:T(8,128)}) custom-call(bf16[64,2048]{1,0:T(8,128)(2,1)} %q_ref.1, bf16[64,2048]{1,0:T(8,128)(2,1)} %d_ref.1, s32[8,128]{1,0:T(8,128)} %tile.12.p_ref), custom_call_target="tpu_custom_call" | custom-call | tf_op jit(solution)/shard_map/step/pallas_call | solution.py:427
  75.4 0.0 copy-start
  75.4 1.9 %copy.7 = f32[64,2048]{1,0:T(8,128)} copy(f32[64,2048]{1,0:T(8,128)} %get-tuple-element.4) | data formatting | bytes 1048576
  77.3 0.0 copy-done
  77.3 0.8 %copy.8 = f32[64,2048]{1,0:T(8,128)} copy(f32[64,2048]{1,0:T(8,128)S(1)} %copy-done) | data formatting | bytes 1048576
Async XLA Ops:
  75.4 1.9 %copy-start = (f32[64,2048]{1,0:T(8,128)S(1)}, f32[64,2048]{1,0:T(8,128)}, u32[]{:S(2)}) copy-start(f32[64,2048]{1,0:T(8,128)} %get-tuple-element.5) | copy-start | bytes 1572868

commit v5 on v4

v5 whole, which is shorter than its diff:
```python
import functools
import jax
import jax.numpy as jnp
from jax import lax
from jax.experimental import pallas as pl
from jax.experimental.pallas import tpu as pltpu
from jax.sharding import Mesh
from jax.sharding import PartitionSpec as P

WIDTHS = 9
LOG2_E = 1.4426950408889634
logit_gain = 3.0

AXES = ("y", "zl", "x", "core", "zh")
MESH = pl.DeviceIdType.MESH
VMEM = pl.BlockSpec(memory_space=pltpu.VMEM)


def width_list(feature_dim):
    return [feature_dim >> WIDTHS - 1 - nested for nested in range(WIDTHS)]


def contract(first_op, second_op, first_dim, second_dim):
    return lax.dot_general(
        first_op,
        second_op,
        (((first_dim,), (second_dim,)), ((), ())),
        preferred_element_type=jnp.float32,
    )


def neighbours(axis):
    size = lax.axis_size(axis)
    me = lax.axis_index(axis)
    up = {axis: lax.rem(me + 1, size)}
    down = {axis: lax.rem(me + size - 1, size)}
    pair = {"zl": 1 - lax.axis_index("zl")}
    if axis == "x":
        pair["zh"] = 1 - lax.axis_index("zh")
    return up, down, pair


def row_peers():
    chips = lax.axis_size("y")
    y = lax.axis_index("y")
    zl = lax.axis_index("zl")
    return [
        (step, pair, {"y": lax.rem(y + step, chips), "zl": lax.rem(zl + pair, 2)})
        for step in range(chips)
        for pair in range(2)
        if step or pair
    ]


def place_of_row(step, pair):
    y = lax.rem(lax.axis_index("y") + step, lax.axis_size("y"))
    return y * 2 + lax.rem(lax.axis_index("zl") + pair, 2)


def place_of_doc(step, pair, other):
    x = lax.rem(lax.axis_index("x") + step, lax.axis_size("x"))
    zh = lax.rem(lax.axis_index("zh") + pair, 2)
    return (x * 2 + zh) * 2 + lax.rem(lax.axis_index("core") + other, 2)


def first_id(place, own):
    x, there, core = place // 4, lax.rem(place // 2, 2), lax.rem(place, 2)
    zl = lax.rem(lax.axis_index("zl") + lax.axis_index("zh") + there, 2)
    chip = (lax.axis_index("y") * 2 + zl) * lax.axis_size("x") + x
    return ((chip * 2 + core) * 2 + there) * own


def meet(devices):
    barrier = pltpu.get_barrier_semaphore()
    for device in devices:
        pl.semaphore_signal(barrier, inc=1, device_id=device, device_id_type=MESH)
    pl.semaphore_wait(barrier, len(devices))


class Sender:
    def __init__(self, sent, landed):
        self.sent, self.landed, self.started = sent, landed, []

    def __call__(self, src, dst, device):
        number = len(self.started)
        copy = pltpu.make_async_remote_copy(
            src_ref=src,
            dst_ref=dst,
            send_sem=self.sent.at[number],
            recv_sem=self.landed.at[number],
            device_id=device,
            device_id_type=MESH,
        )
        copy.start()
        self.started.append(copy)
        return copy

    def finish(self):
        for copy in self.started:
            copy.wait_send()


def gather(send, q_ref, d_ref, rows_ref, docs_ref):
    own = q_ref.shape[0]
    half = own // 2
    sibling = {"core": 1 - lax.axis_index("core")}

    def q_slot(step, pair, lo=0, size=own):
        start = place_of_row(step, pair) * own + lo
        return rows_ref.at[pl.ds(pl.multiple_of(start, half), size), :]

    def d_slot(step, pair, lo=0, size=own):
        start = place_of_doc(step, pair, 0) * own + lo
        return docs_ref.at[pl.ds(pl.multiple_of(start, half), size), :]

    lanes = ((q_ref, q_slot, *neighbours("y")), (d_ref, d_slot, *neighbours("x")))
    first = [
        tuple(send(src, slot(0, 0), device) for device in (pair, up, down))
        for src, slot, up, down, pair in lanes
    ]
    across = [send(d_ref, d_slot(0, 0), sibling)]
    rows_ref[pl.ds(pl.multiple_of(place_of_row(0, 0) * own, own), own), :] = q_ref[...]
    docs_ref[pl.ds(pl.multiple_of(place_of_doc(0, 0, 0) * own, own), own), :] = d_ref[...]
    second = []
    for (src, slot, up, down, _), copies in zip(lanes, first):
        copies[0].wait_recv()
        second.append(tuple(send(slot(0, 1), slot(0, 1), device) for device in (up, down)))
    across.append(send(d_slot(0, 1), d_slot(0, 1), sibling))
    far = []
    for pair, stage in ((0, first), (1, second)):
        for (src, slot, up, down, _), copies in zip(lanes, stage):
            for copy, step, device, lo in ((copies[-2], 3, up, 0), (copies[-1], 1, down, half)):
                copy.wait_recv()
                piece = slot(step, pair, lo, half)
                far.append(send(piece, piece, device))
        for step in (3, 1):
            across.append(send(d_slot(step, pair), d_slot(step, pair), sibling))
    for copy in far:
        copy.wait_recv()
    for pair in range(2):
        across.append(send(d_slot(2, pair), d_slot(2, pair), sibling))
    for copy in across:
        copy.wait_recv()


def step_kernel(
    q_ref,
    d_ref,
    p_ref,
    gq_ref,
    gd_ref,
    rows_ref,
    docs_ref,
    logits,
    bands,
    best,
    mass,
    peaks,
    lse,
    parts,
    marks,
    pq_ref,
    pd_ref,
    sib,
    far_s,
    near_s,
    far_r,
    near_r,
    pair_s,
    pair_r,
    sent,
    landed,
):
    count, dim = docs_ref.shape
    width = rows_ref.shape[0]
    own = q_ref.shape[0]
    half = own // 2
    uppers = width_list(dim)
    lowers = [0] + uppers[:-1]
    scales = [logit_gain * upper ** (-0.5) for upper in uppers]
    narrow = 256
    few = uppers.index(narrow) + 1
    chips = lax.axis_size("y")
    sibling = {"core": 1 - lax.axis_index("core")}
    meet([device for _, _, device in row_peers()] + [*neighbours("x"), sibling])
    send = Sender(sent, landed)

    marked = [send(p_ref, marks.at[place_of_row(0, 0)], device) for _, _, device in row_peers()]
    marks[place_of_row(0, 0)] = p_ref[...]
    lse[...] = jnp.zeros_like(lse)
    peaks[...] = jnp.zeros_like(peaks)
    gather(send, q_ref, d_ref, rows_ref, docs_ref)
    for copy in marked:
        copy.wait_recv()
    side = lax.broadcasted_iota(jnp.int32, (1, 2 * own), 1)
    partner = jnp.concatenate(
        [
            jnp.where(side < own, marks[2 * step, 0:1, :], marks[2 * step + 1, 0:1, :])
            for step in range(chips)
        ],
        axis=1,
    )

    turn = width // 2
    tall = count // 2

    def turn_cols(part, nested=0):
        start = nested * width + part * turn
        return slice(start, start + turn)

    def score(part):
        cols_q = turn_cols(part)
        best[...] = jnp.full(best.shape, -jnp.inf, jnp.float32)

        def keep(nested, at, value):
            logits[nested, at, cols_q] = value
            top = jnp.max(value.reshape(tall // 8, 8, turn), axis=0)
            best[nested] = jnp.maximum(best[nested], top)

        def score_block(block, carry):
            at = pl.ds(pl.multiple_of(block * tall, tall), tall)
            lane = lax.broadcasted_iota(jnp.int32, (tall, narrow), 1)
            head = docs_ref[at, :narrow]
            for nested in range(few):
                cut = jnp.where(lane < uppers[nested], head, jnp.zeros_like(head))
                keep(nested, at, contract(cut, rows_ref[cols_q, :narrow], 1, 1))
            for nested in range(few, WIDTHS):
                cols = slice(lowers[nested], uppers[nested])
                more = contract(docs_ref[at, cols], rows_ref[cols_q, cols], 1, 1)
                keep(nested, at, logits[nested - 1, at, cols_q] + more)
            return carry

        lax.fori_loop(0, count // tall, score_block, 0)

    def soften(part):
        cols_q = turn_cols(part)
        tops = [jnp.max(best[nested], axis=0, keepdims=True) for nested in range(WIDTHS)]
        mass[...] = jnp.zeros_like(mass)
        size = 128

        def mass_block(block, carry):
            at = pl.ds(pl.multiple_of(block * size, size), size)
            for nested in range(WIDTHS):
                piece = logits[nested, at, cols_q] - tops[nested]
                piece = jnp.exp2(piece * (scales[nested] * LOG2_E))
                logits[nested, at, cols_q] = piece
                mass[nested] += jnp.sum(piece.reshape(size // 8, 8, turn), axis=0)
            return carry

        lax.fori_loop(0, count // size, mass_block, 0)
        for nested in range(WIDTHS):
            top = tops[nested] * scales[nested]
            value = top + jnp.log(jnp.sum(mass[nested], axis=0, keepdims=True))
            if nested < 8:
                peaks[part, nested : nested + 1, :turn] = top
                lse[part, nested : nested + 1, :turn] = value
            else:
                for line in range(turn // 128):
                    cols = slice(line * 128, (line + 1) * 128)
                    peaks[part, line : line + 1, turn:] = top[:, cols]
                    lse[part, line : line + 1, turn:] = value[:, cols]

    def share(part):
        return [
            send(lse.at[part], parts.at[part, (chips - step) % chips * 2 + pair - 1], device)
            for step, pair, device in row_peers()
        ]

    def factors(part, copies):
        for copy in copies:
            copy.wait_recv()
        pieces = [lse[part]] + [parts[part, number] for number in range(len(copies))]
        peak = functools.reduce(jnp.maximum, pieces)
        total = peak + jnp.log(sum(jnp.exp(piece - peak) for piece in pieces))
        ratio = jnp.exp(peaks[part] - total)
        rows = [ratio[nested : nested + 1, :turn] * scales[nested] for nested in range(8)]
        tail = [ratio[line : line + 1, turn:] for line in range(turn // 128)]
        return rows + [jnp.concatenate(tail, axis=1) * scales[8]]

    def band(part, factor):
        cols_q = turn_cols(part)

        def band_block(block, carry):
            at = pl.ds(pl.multiple_of(block * own, own), own)
            ids = first_id(block, own) + lax.broadcasted_iota(jnp.int32, (own, turn), 0)
            hit = ids == partner[:, cols_q]
            running = jnp.zeros((own, turn), jnp.float32)
            gone = 0.0
            for nested in reversed(range(WIDTHS)):
                running = running + logits[nested, at, cols_q] * factor[nested]
                gone += scales[nested]
                value = running - jnp.where(hit, gone, 0.0)
                bands[at, turn_cols(part, nested)] = value.astype(jnp.bfloat16)
            return carry

        lax.fori_loop(0, count // own, band_block, 0)

    def bounds(nested):
        return slice(0, narrow) if nested < few else slice(lowers[nested], uppers[nested])

    def product(tall_rows, get, out_ref, at):
        lane = lax.broadcasted_iota(jnp.int32, (tall_rows, narrow), 1)
        head = None
        for nested in range(WIDTHS):
            part = get(nested, bounds(nested))
            if nested < few:
                head = part if head is None else jnp.where(lane < lowers[nested], head, part)
                part = head
            if nested >= few - 1:
                out_ref[at, bounds(nested)] = part

    across = {}

    def d_rows(step, pair, other, lo=0, size=own):
        start = place_of_doc(step, pair, other) * own + lo
        return pl.ds(pl.multiple_of(start, half), size)

    def documents_for(step):
        piece = 4 * own
        chip = lax.rem(lax.axis_index("x") + step, chips)
        at = pl.ds(pl.multiple_of(chip * piece, piece), piece)
        product(
            piece,
            lambda nested, cols: contract(
                bands[at, nested * width : (nested + 1) * width], rows_ref[:, cols], 1, 0
            ),
            pd_ref,
            at,
        )
        for pair in (1, 0):
            theirs = pd_ref.at[d_rows(step, pair, 1), :]
            across[step, pair] = send(theirs, sib.at[step * 2 + pair], sibling)

    def queries_at(chip):
        piece = 2 * own
        product(
            piece,
            lambda nested, cols: contract(
                bands[:, nested * width + chip * piece : nested * width + (chip + 1) * piece],
                docs_ref[:, cols],
                0,
                0,
            ),
            pq_ref,
            slice(chip * piece, (chip + 1) * piece),
        )

    def q_part(step, pair, lo=0, size=own):
        start = place_of_row(step, pair) * own + lo
        return pq_ref[pl.ds(pl.multiple_of(start, half), size), :]

    def d_part(step, pair, lo=0, size=own):
        return pd_ref[d_rows(step, pair, 0, lo, size), :] + sib[step * 2 + pair, pl.ds(lo, size), :]

    lanes = ((q_part, *neighbours("y")), (d_part, *neighbours("x")))
    far = {}
    near = {}

    def send_far(which, pair):
        part, up, down, _ = lanes[which]
        far_s[which, pair] = part(2, pair).astype(jnp.bfloat16)
        for way, device in ((0, up), (1, down)):
            piece = pl.ds(way * half, half)
            far[which, pair, way] = send(
                far_s.at[which, pair, piece], far_r.at[which, pair, piece], device
            )

    def send_near(which, pair):
        part, up, down, _ = lanes[which]
        for way, device, step in ((0, up, 1), (1, down, 3)):
            if which == 1:
                across[step, pair].wait_recv()
            far[which, pair, way].wait_recv()
            lo = way * half
            more = half - lo
            near_s[which, pair, way, pl.ds(lo, half), :] = (
                part(step, pair, lo, half)
                + far_r[which, pair, pl.ds(lo, half), :].astype(jnp.float32)
            ).astype(jnp.bfloat16)
            near_s[which, pair, way, pl.ds(more, half), :] = part(step, pair, more, half).astype(
                jnp.bfloat16
            )
            near[which, pair, way] = send(
                near_s.at[which, pair, way], near_r.at[which, pair, way], device
            )

    def arrived(which, pair):
        part = lanes[which][0]
        if which == 1:
            across[0, pair].wait_recv()
        near[which, pair, 0].wait_recv()
        near[which, pair, 1].wait_recv()
        return (
            part(0, pair)
            + near_r[which, pair, 0].astype(jnp.float32)
            + near_r[which, pair, 1].astype(jnp.float32)
        )

    shared = []
    for part in range(2):
        score(part)
        soften(part)
        shared.append(share(part))
    band(0, factors(0, shared[0]))
    queries_at(0)
    queries_at(1)
    band(1, factors(1, shared[1]))
    documents_for(2)
    queries_at(2)
    queries_at(3)
    send_far(0, 1)
    send_far(0, 0)
    for pair in (1, 0):
        across[2, pair].wait_recv()
        send_far(1, pair)
    documents_for(1)
    documents_for(3)
    for pair in (1, 0):
        send_near(0, pair)
        send_near(1, pair)
    documents_for(0)
    last = []
    for which in range(2):
        pair_s[which] = arrived(which, 1).astype(jnp.bfloat16)
        last.append(send(pair_s.at[which], pair_r.at[which], lanes[which][3]))
    outs = (gq_ref, gd_ref)
    for which in range(2):
        outs[which][...] = arrived(which, 0)
    for which in range(2):
        last[which].wait_recv()
        outs[which][...] = outs[which][...] + pair_r[which].astype(jnp.float32)
    send.finish()


def on_device(queries, documents, partner):
    own, dim = queries.shape
    width, count = 8 * own, 16 * own
    piece = jax.ShapeDtypeStruct((own, dim), jnp.float32)
    wire = jnp.bfloat16
    copies = 7 + 26 + 14 + 30
    return pl.pallas_call(
        step_kernel,
        out_shape=(piece, piece),
        in_specs=[VMEM] * 3,
        out_specs=(VMEM, VMEM),
        scratch_shapes=[
            pltpu.VMEM((width, dim), wire),
            pltpu.VMEM((count, dim), wire),
            pltpu.VMEM((WIDTHS, count, width), jnp.float32),
            pltpu.VMEM((count, WIDTHS * width), wire),
            pltpu.VMEM((WIDTHS, 8, width // 2), jnp.float32),
            pltpu.VMEM((WIDTHS, 8, width // 2), jnp.float32),
            pltpu.VMEM((2, 8, width // 2 + 128), jnp.float32),
            pltpu.VMEM((2, 8, width // 2 + 128), jnp.float32),
            pltpu.VMEM((2, 7, 8, width // 2 + 128), jnp.float32),
            pltpu.VMEM((8, 8, 2 * own), jnp.int32),
            pltpu.VMEM((width, dim), jnp.float32),
            pltpu.VMEM((count, dim), jnp.float32),
            pltpu.VMEM((8, own, dim), jnp.float32),
            pltpu.VMEM((2, 2, own, dim), wire),
            pltpu.VMEM((2, 2, 2, own, dim), wire),
            pltpu.VMEM((2, 2, own, dim), wire),
            pltpu.VMEM((2, 2, 2, own, dim), wire),
            pltpu.VMEM((2, own, dim), wire),
            pltpu.VMEM((2, own, dim), wire),
            pltpu.SemaphoreType.DMA((copies,)),
            pltpu.SemaphoreType.DMA((copies,)),
        ],
        compiler_params=pltpu.CompilerParams(
            collective_id=0, has_side_effects=True, vmem_limit_bytes=67043328
        ),
        name="step",
    )(queries, documents, jnp.tile(partner[None, :], (8, 2)))


def solution(mesh):
    finer = Mesh(mesh.devices.reshape(4, 2, 4, 2, mesh.shape["rep"]), AXES)
    placed = (P(AXES, None), P(AXES, None), P(AXES))
    return jax.shard_map(
        on_device,
        mesh=finer,
        in_specs=placed,
        out_specs=(P(AXES, None), P(AXES, None)),
        check_vma=False,
    )
```

time: 79.1 us -> 76.8 us (0.971)
  Pallas kernels: 73.4 us -> 71.9 us
    pallas_call x1, Pallas kernels: 73.4 us -> 71.9 us  [on_device(): pl.pallas_call(step_kernel, out_shape=(piece, piece), in_specs=[VMEM] * 3...]
where the time goes in v5:
time: 76.8 us; the launch traced here: 76.6 us
  Pallas kernels  71.9 us (94%)
  local copies, waits for them, and re-layouts  4.06 us (5%)
    pallas_call x1, Pallas kernels, on_device(): pl.pallas_call(step_kernel, out_shape=(piece, piece), in_specs=[VMEM] * 3...  71.9 us
    unnamed x4, local copies, waits for them, and re-layouts  2.73 us

profile of v5, /device:TPU:1, one launch (start us, length us, event | category | flops | bytes accessed | tf_op | source)
XLA Modules:
  0.0 76.6 jit_solution(5006673896858111499)
XLA Ops:
  0.6 0.7 tile.10
  1.3 0.1 tile.11
  1.4 0.6 tile.12.p_ref
  2.0 71.9 %step.1 = (f32[64,2048]{1,0:T(8,128)}, f32[64,2048]{1,0:T(8,128)}) custom-call(bf16[64,2048]{1,0:T(8,128)(2,1)} %q_ref.1, bf16[64,2048]{1,0:T(8,128)(2,1)} %d_ref.1, s32[8,128]{1,0:T(8,128)} %tile.12.p_ref), custom_call_target="tpu_custom_call" | custom-call | tf_op jit(solution)/shard_map/step/pallas_call | solution.py:441
  73.9 0.0 copy-start
  73.9 1.9 %copy.7 = f32[64,2048]{1,0:T(8,128)} copy(f32[64,2048]{1,0:T(8,128)} %get-tuple-element.4) | data formatting | bytes 1048576
  75.8 0.0 copy-done
  75.8 0.8 %copy.8 = f32[64,2048]{1,0:T(8,128)} copy(f32[64,2048]{1,0:T(8,128)S(1)} %copy-done) | data formatting | bytes 1048576
Async XLA Ops:
  73.9 1.9 %copy-start = (f32[64,2048]{1,0:T(8,128)S(1)}, f32[64,2048]{1,0:T(8,128)}, u32[]{:S(2)}) copy-start(f32[64,2048]{1,0:T(8,128)} %get-tuple-element.5) | copy-start | bytes 1572868

commit v6 on v5

--- a/solution.py
+++ b/solution.py
@@ -18,6 +18,10 @@
 
 def width_list(feature_dim):
     return [feature_dim >> WIDTHS - 1 - nested for nested in range(WIDTHS)]
+
+
+def split_at(dim):
+    return dim * 9 // 16
 
 
 def contract(first_op, second_op, first_dim, second_dim):
@@ -100,45 +104,84 @@
             copy.wait_send()
 
 
-def gather(send, q_ref, d_ref, rows_ref, docs_ref):
-    own = q_ref.shape[0]
+def gather(send, rows_ref, docs_ref, own):
     half = own // 2
     sibling = {"core": 1 - lax.axis_index("core")}
-
-    def q_slot(step, pair, lo=0, size=own):
+    dim = docs_ref.shape[1]
+    early, late, every = slice(0, split_at(dim)), slice(split_at(dim), dim), slice(0, dim)
+
+    def q_slot(step, pair, cols, lo=0, size=own):
         start = place_of_row(step, pair) * own + lo
-        return rows_ref.at[pl.ds(pl.multiple_of(start, half), size), :]
-
-    def d_slot(step, pair, lo=0, size=own):
+        return rows_ref.at[pl.ds(pl.multiple_of(start, half), size), cols]
+
+    def d_slot(step, pair, cols, lo=0, size=own):
         start = place_of_doc(step, pair, 0) * own + lo
-        return docs_ref.at[pl.ds(pl.multiple_of(start, half), size), :]
-
-    lanes = ((q_ref, q_slot, *neighbours("y")), (d_ref, d_slot, *neighbours("x")))
-    first = [
-        tuple(send(src, slot(0, 0), device) for device in (pair, up, down))
-        for src, slot, up, down, pair in lanes
-    ]
-    across = [send(d_ref, d_slot(0, 0), sibling)]
-    rows_ref[pl.ds(pl.multiple_of(place_of_row(0, 0) * own, own), own), :] = q_ref[...]
-    docs_ref[pl.ds(pl.multiple_of(place_of_doc(0, 0, 0) * own, own), own), :] = d_ref[...]
-    second = []
-    for (src, slot, up, down, _), copies in zip(lanes, first):
-        copies[0].wait_recv()
-        second.append(tuple(send(slot(0, 1), slot(0, 1), device) for device in (up, down)))
-    across.append(send(d_slot(0, 1), d_slot(0, 1), sibling))
-    far = []
-    for pair, stage in ((0, first), (1, second)):
-        for (src, slot, up, down, _), copies in zip(lanes, stage):
-            for copy, step, device, lo in ((copies[-2], 3, up, 0), (copies[-1], 1, down, half)):
-                copy.wait_recv()
-                piece = slot(step, pair, lo, half)
-                far.append(send(piece, piece, device))
-        for step in (3, 1):
-            across.append(send(d_slot(step, pair), d_slot(step, pair), sibling))
-    for copy in far:
-        copy.wait_recv()
-    for pair in range(2):
-        across.append(send(d_slot(2, pair), d_slot(2, pair), sibling))
+        return docs_ref.at[pl.ds(pl.multiple_of(start, half), size), cols]
+
+    lanes = ((d_slot, *neighbours("x")), (q_slot, *neighbours("y")))
+    across = []
+
+    def cross(which, step, pair, cols):
+        if which == 0:
+            piece = d_slot(step, pair, cols)
+            across.append(send(piece, piece, sibling))
+
+    def onward(piece, device):
+        return send(piece, piece, device)
+
+    own_early, own_late, up_late, down_late, up_early, down_early = ([] for _ in range(6))
+    for slot, up, down, pair in lanes:
+        own_early.append(onward(slot(0, 0, early), pair))
+        up_late.append(onward(slot(0, 0, late), up))
+        down_late.append(onward(slot(0, 0, late), down))
+        up_early.append(onward(slot(0, 0, early), up))
+        down_early.append(onward(slot(0, 0, early), down))
+        own_late.append(onward(slot(0, 0, late), pair))
+    cross(0, 0, 0, every)
+
+    def relay(which, step_pair, cols, copies):
+        slot, up, down, _ = lanes[which]
+        from_down, from_up = copies
+        from_down.wait_recv()
+        first = onward(slot(3, step_pair, cols, 0, half), up)
+        from_up.wait_recv()
+        return first, onward(slot(1, step_pair, cols, half, half), down)
+
+    far_late, back_late, beside, far_early, far_pair, last_late = ([] for _ in range(6))
+    for which, (slot, up, down, pair) in enumerate(lanes):
+        far_late.append(relay(which, 0, late, (up_late[which], down_late[which])))
+        back_late.append([onward(slot(step, 0, late), pair) for step in (3, 1)])
+    for which, (slot, up, down, pair) in enumerate(lanes):
+        own_early[which].wait_recv()
+        beside.append([onward(slot(0, 1, early), device) for device in (up, down)])
+        cross(which, 0, 1, early)
+    for which in range(2):
+        far_early.append(relay(which, 0, early, (up_early[which], down_early[which])))
+        cross(which, 3, 0, every)
+        cross(which, 1, 0, every)
+    for which, (slot, up, down, pair) in enumerate(lanes):
+        for copy in far_late[which]:
+            copy.wait_recv()
+        last_late.append(onward(slot(2, 0, late), pair))
+        cross(which, 2, 0, late)
+        own_late[which].wait_recv()
+        cross(which, 0, 1, late)
+    for which in range(2):
+        far_pair.append(relay(which, 1, early, beside[which]))
+        for copy in back_late[which]:
+            copy.wait_recv()
+        cross(which, 3, 1, every)
+        cross(which, 1, 1, every)
+    for which in range(2):
+        for copy in far_early[which]:
+            copy.wait_recv()
+        cross(which, 2, 0, early)
+    for which in range(2):
+        last_late[which].wait_recv()
+        cross(which, 2, 1, late)
+        for copy in far_pair[which]:
+            copy.wait_recv()
+        cross(which, 2, 1, early)
     for copy in across:
         copy.wait_recv()
 
@@ -168,6 +211,9 @@
     near_r,
     pair_s,
     pair_r,
+    cross_s,
+    cross_r,
+    inside,
     sent,
     landed,
 ):
@@ -182,24 +228,24 @@
     few = uppers.index(narrow) + 1
     chips = lax.axis_size("y")
     sibling = {"core": 1 - lax.axis_index("core")}
-    meet([device for _, _, device in row_peers()] + [*neighbours("x"), sibling])
     send = Sender(sent, landed)
 
-    marked = [send(p_ref, marks.at[place_of_row(0, 0)], device) for _, _, device in row_peers()]
+    q_place = pl.ds(pl.multiple_of(place_of_row(0, 0) * own, own), own)
+    d_place = pl.ds(pl.multiple_of(place_of_doc(0, 0, 0) * own, own), own)
+    taken = [
+        pltpu.make_async_copy(d_ref, docs_ref.at[d_place, :], inside.at[0]),
+        pltpu.make_async_copy(q_ref, rows_ref.at[q_place, :], inside.at[1]),
+    ]
+    for copy in taken:
+        copy.start()
+    meet([*neighbours("y"), *neighbours("x"), sibling])
+    for copy in taken:
+        copy.wait()
     marks[place_of_row(0, 0)] = p_ref[...]
     lse[...] = jnp.zeros_like(lse)
     peaks[...] = jnp.zeros_like(peaks)
-    gather(send, q_ref, d_ref, rows_ref, docs_ref)
-    for copy in marked:
-        copy.wait_recv()
-    side = lax.broadcasted_iota(jnp.int32, (1, 2 * own), 1)
-    partner = jnp.concatenate(
-        [
-            jnp.where(side < own, marks[2 * step, 0:1, :], marks[2 * step + 1, 0:1, :])
-            for step in range(chips)
-        ],
-        axis=1,
-    )
+    gather(send, rows_ref, docs_ref, own)
+    marked = [send(p_ref, marks.at[place_of_row(0, 0)], device) for _, _, device in row_peers()]
 
     turn = width // 2
     tall = count // 2
@@ -277,7 +323,7 @@
         tail = [ratio[line : line + 1, turn:] for line in range(turn // 128)]
         return rows + [jnp.concatenate(tail, axis=1) * scales[8]]
 
-    def band(part, factor):
+    def band(part, factor, partner):
         cols_q = turn_cols(part)
 
         def band_block(block, carry):
@@ -345,90 +391,126 @@
             slice(chip * piece, (chip + 1) * piece),
         )
 
-    def q_part(step, pair, lo=0, size=own):
+    def q_part(step, pair, lo, size, cols):
         start = place_of_row(step, pair) * own + lo
-        return pq_ref[pl.ds(pl.multiple_of(start, half), size), :]
-
-    def d_part(step, pair, lo=0, size=own):
-        return pd_ref[d_rows(step, pair, 0, lo, size), :] + sib[step * 2 + pair, pl.ds(lo, size), :]
+        return pq_ref[pl.ds(pl.multiple_of(start, half), size), cols]
+
+    def d_part(step, pair, lo, size, cols):
+        arrive(across[step, pair])
+        mine = pd_ref[d_rows(step, pair, 0, lo, size), cols]
+        return mine + sib[step * 2 + pair, pl.ds(lo, size), cols]
+
+    waited = []
+
+    def arrive(copy):
+        if not any(copy is seen for seen in waited):
+            copy.wait_recv()
+            waited.append(copy)
 
     lanes = ((q_part, *neighbours("y")), (d_part, *neighbours("x")))
-    far = {}
-    near = {}
-
-    def send_far(which, pair):
-        part, up, down, _ = lanes[which]
-        far_s[which, pair] = part(2, pair).astype(jnp.bfloat16)
+    edge = split_at(dim)
+    early, late = slice(0, edge), slice(edge, dim)
+    crossed, far, near = {}, {}, {}
+
+    def cross(which, step):
+        part, _, _, pair = lanes[which]
+        cross_s[which, step] = part(step, 1, 0, own, late).astype(jnp.bfloat16)
+        crossed[which, step] = send(cross_s.at[which, step], cross_r.at[which, step], pair)
+
+    def term(which, pair, cols, step, lo, size):
+        value = lanes[which][0](step, pair, lo, size, cols)
+        if cols is late:
+            arrive(crossed[which, step])
+            value = value + cross_r[which, step, pl.ds(lo, size), :].astype(jnp.float32)
+        return value
+
+    def send_far(which, pair, cols):
+        _, up, down, _ = lanes[which]
+        far_s[which, pair, :, cols] = term(which, pair, cols, 2, 0, own).astype(jnp.bfloat16)
         for way, device in ((0, up), (1, down)):
             piece = pl.ds(way * half, half)
-            far[which, pair, way] = send(
-                far_s.at[which, pair, piece], far_r.at[which, pair, piece], device
+            far[which, pair, cols.start, way] = send(
+                far_s.at[which, pair, piece, cols], far_r.at[which, pair, piece, cols], device
             )
 
-    def send_near(which, pair):
-        part, up, down, _ = lanes[which]
+    def send_near(which, pair, cols):
+        _, up, down, _ = lanes[which]
         for way, device, step in ((0, up, 1), (1, down, 3)):
-            if which == 1:
-                across[step, pair].wait_recv()
-            far[which, pair, way].wait_recv()
             lo = way * half
             more = half - lo
-            near_s[which, pair, way, pl.ds(lo, half), :] = (
-                part(step, pair, lo, half)
-                + far_r[which, pair, pl.ds(lo, half), :].astype(jnp.float32)
+            near_s[which, pair, way, pl.ds(more, half), cols] = term(
+                which, pair, cols, step, more, half
             ).astype(jnp.bfloat16)
-            near_s[which, pair, way, pl.ds(more, half), :] = part(step, pair, more, half).astype(
-                jnp.bfloat16
+            mine = term(which, pair, cols, step, lo, half)
+            arrive(far[which, pair, cols.start, way])
+            near_s[which, pair, way, pl.ds(lo, half), cols] = (
+                mine + far_r[which, pair, pl.ds(lo, half), cols].astype(jnp.float32)
+            ).astype(jnp.bfloat16)
+            near[which, pair, cols.start, way] = send(
+                near_s.at[which, pair, way, :, cols], near_r.at[which, pair, way, :, cols], device
             )
-            near[which, pair, way] = send(
-                near_s.at[which, pair, way], near_r.at[which, pair, way], device
-            )
-
-    def arrived(which, pair):
-        part = lanes[which][0]
-        if which == 1:
-            across[0, pair].wait_recv()
-        near[which, pair, 0].wait_recv()
-        near[which, pair, 1].wait_recv()
-        return (
-            part(0, pair)
-            + near_r[which, pair, 0].astype(jnp.float32)
-            + near_r[which, pair, 1].astype(jnp.float32)
-        )
+
+    def summed(which, pair, cols):
+        value = term(which, pair, cols, 0, 0, own)
+        for way in range(2):
+            arrive(near[which, pair, cols.start, way])
+            value = value + near_r[which, pair, way, :, cols].astype(jnp.float32)
+        return value
 
     shared = []
     for part in range(2):
         score(part)
         soften(part)
         shared.append(share(part))
-    band(0, factors(0, shared[0]))
+    for copy in marked:
+        copy.wait_recv()
+    side = lax.broadcasted_iota(jnp.int32, (1, 2 * own), 1)
+    partner = jnp.concatenate(
+        [
+            jnp.where(side < own, marks[2 * step, 0:1, :], marks[2 * step + 1, 0:1, :])
+            for step in range(chips)
+        ],
+        axis=1,
+    )
+    band(0, factors(0, shared[0]), partner)
     queries_at(0)
     queries_at(1)
-    band(1, factors(1, shared[1]))
+    band(1, factors(1, shared[1]), partner)
     documents_for(2)
     queries_at(2)
     queries_at(3)
-    send_far(0, 1)
-    send_far(0, 0)
-    for pair in (1, 0):
-        across[2, pair].wait_recv()
-        send_far(1, pair)
+    for which in range(2):
+        cross(which, 2)
+        send_far(which, 1, early)
+        send_far(which, 0, early)
+    for step in (1, 3, 0):
+        cross(0, step)
     documents_for(1)
     documents_for(3)
-    for pair in (1, 0):
-        send_near(0, pair)
-        send_near(1, pair)
+    for which in range(2):
+        send_far(which, 0, late)
+    cross(1, 1)
+    cross(1, 3)
+    for which in range(2):
+        send_near(which, 1, early)
     documents_for(0)
+    for which in range(2):
+        send_near(which, 0, early)
+    cross(1, 0)
+    for which in range(2):
+        send_near(which, 0, late)
+    outs = (gq_ref, gd_ref)
     last = []
     for which in range(2):
-        pair_s[which] = arrived(which, 1).astype(jnp.bfloat16)
+        pair_s[which] = summed(which, 1, early).astype(jnp.bfloat16)
         last.append(send(pair_s.at[which], pair_r.at[which], lanes[which][3]))
-    outs = (gq_ref, gd_ref)
-    for which in range(2):
-        outs[which][...] = arrived(which, 0)
+    for which in range(2):
+        outs[which][:, early] = summed(which, 0, early)
+    for which in range(2):
+        outs[which][:, late] = summed(which, 0, late)
     for which in range(2):
         last[which].wait_recv()
-        outs[which][...] = outs[which][...] + pair_r[which].astype(jnp.float32)
+        outs[which][:, early] = outs[which][:, early] + pair_r[which].astype(jnp.float32)
     send.finish()
 
 
@@ -437,11 +519,12 @@
     width, count = 8 * own, 16 * own
     piece = jax.ShapeDtypeStruct((own, dim), jnp.float32)
     wire = jnp.bfloat16
-    copies = 7 + 26 + 14 + 30
+    edge = split_at(dim)
+    copies = 120
     return pl.pallas_call(
         step_kernel,
         out_shape=(piece, piece),
-        in_specs=[VMEM] * 3,
+        in_specs=[pl.BlockSpec(memory_space=pl.ANY)] * 2 + [VMEM],
         out_specs=(VMEM, VMEM),
         scratch_shapes=[
             pltpu.VMEM((width, dim), wire),
@@ -461,8 +544,11 @@
             pltpu.VMEM((2, 2, 2, own, dim), wire),
             pltpu.VMEM((2, 2, own, dim), wire),
             pltpu.VMEM((2, 2, 2, own, dim), wire),
-            pltpu.VMEM((2, own, dim), wire),
-            pltpu.VMEM((2, own, dim), wire),
+            pltpu.VMEM((2, own, edge), wire),
+            pltpu.VMEM((2, own, edge), wire),
+            pltpu.VMEM((2, 4, own, dim - edge), wire),
+            pltpu.VMEM((2, 4, own, dim - edge), wire),
+            pltpu.SemaphoreType.DMA((2,)),
             pltpu.SemaphoreType.DMA((copies,)),
             pltpu.SemaphoreType.DMA((copies,)),
         ],

time: 76.8 us -> 67.4 us (0.88)
  Pallas kernels: 71.9 us -> 62.2 us
    pallas_call x1, Pallas kernels: 71.9 us -> 62.2 us  [on_device(): pl.pallas_call(step_kernel, out_shape=(piece, piece), in_specs=[pl.BlockS...]
where the time goes in v6:
time: 67.4 us; the launch traced here: 66.9 us
  Pallas kernels  62.2 us (92%)
  local copies, waits for them, and re-layouts  4.06 us (6%)
    pallas_call x1, Pallas kernels, on_device(): pl.pallas_call(step_kernel, out_shape=(piece, piece), in_specs=[pl.BlockS...  62.2 us
    unnamed x4, local copies, waits for them, and re-layouts  2.73 us

profile of v6, /device:TPU:1, one launch (start us, length us, event | category | flops | bytes accessed | tf_op | source)
XLA Modules:
  0.0 66.9 jit_solution(8412712172559642150)
XLA Ops:
  0.6 0.7 tile.10
  1.3 0.1 tile.11
  1.4 0.6 tile.12.p_ref
  2.0 62.2 %step.1 = (f32[64,2048]{1,0:T(8,128)}, f32[64,2048]{1,0:T(8,128)}) custom-call(bf16[64,2048]{1,0:T(8,128)(2,1)} %q_ref.1, bf16[64,2048]{1,0:T(8,128)(2,1)} %d_ref.1, s32[8,128]{1,0:T(8,128)} %tile.12.p_ref), custom_call_target="tpu_custom_call" | custom-call | tf_op jit(solution)/shard_map/step/pallas_call | solution.py:524
  64.1 0.0 copy-start
  64.1 1.9 %copy.7 = f32[64,2048]{1,0:T(8,128)} copy(f32[64,2048]{1,0:T(8,128)} %get-tuple-element.4) | data formatting | bytes 1048576
  66.1 0.0 copy-done
  66.1 0.8 %copy.8 = f32[64,2048]{1,0:T(8,128)} copy(f32[64,2048]{1,0:T(8,128)S(1)} %copy-done) | data formatting | bytes 1048576
Async XLA Ops:
  64.1 1.9 %copy-start = (f32[64,2048]{1,0:T(8,128)S(1)}, f32[64,2048]{1,0:T(8,128)}, u32[]{:S(2)}) copy-start(f32[64,2048]{1,0:T(8,128)} %get-tuple-element.5) | copy-start | bytes 1572868

commit v7 on v6

--- a/solution.py
+++ b/solution.py
@@ -382,13 +382,13 @@
         product(
             piece,
             lambda nested, cols: contract(
-                bands[:, nested * width + chip * piece : nested * width + (chip + 1) * piece],
+                bands[:, pl.ds(pl.multiple_of(nested * width + chip * piece, piece), piece)],
                 docs_ref[:, cols],
                 0,
                 0,
             ),
             pq_ref,
-            slice(chip * piece, (chip + 1) * piece),
+            pl.ds(pl.multiple_of(chip * piece, piece), piece),
         )
 
     def q_part(step, pair, lo, size, cols):
@@ -464,25 +464,21 @@
         shared.append(share(part))
     for copy in marked:
         copy.wait_recv()
-    side = lax.broadcasted_iota(jnp.int32, (1, 2 * own), 1)
-    partner = jnp.concatenate(
-        [
-            jnp.where(side < own, marks[2 * step, 0:1, :], marks[2 * step + 1, 0:1, :])
-            for step in range(chips)
-        ],
-        axis=1,
-    )
+    partner = jnp.concatenate([marks[place] for place in range(2 * chips)], axis=1)
     band(0, factors(0, shared[0]), partner)
     queries_at(0)
     queries_at(1)
     band(1, factors(1, shared[1]), partner)
     documents_for(2)
-    queries_at(2)
-    queries_at(3)
-    for which in range(2):
-        cross(which, 2)
-        send_far(which, 1, early)
-        send_far(which, 0, early)
+    odd = lax.rem(lax.axis_index("y"), 2)
+    queries_at(2 + odd)
+    cross(0, 2)
+    send_far(0, 1, early)
+    send_far(0, 0, early)
+    queries_at(3 - odd)
+    cross(1, 2)
+    send_far(1, 1, early)
+    send_far(1, 0, early)
     for step in (1, 3, 0):
         cross(0, step)
     documents_for(1)
@@ -517,7 +513,7 @@
 def on_device(queries, documents, partner):
     own, dim = queries.shape
     width, count = 8 * own, 16 * own
-    piece = jax.ShapeDtypeStruct((own, dim), jnp.float32)
+    piece = pltpu.VMEM((own, dim), jnp.float32)
     wire = jnp.bfloat16
     edge = split_at(dim)
     copies = 120
@@ -536,7 +532,7 @@
             pltpu.VMEM((2, 8, width // 2 + 128), jnp.float32),
             pltpu.VMEM((2, 8, width // 2 + 128), jnp.float32),
             pltpu.VMEM((2, 7, 8, width // 2 + 128), jnp.float32),
-            pltpu.VMEM((8, 8, 2 * own), jnp.int32),
+            pltpu.VMEM((8, 1, own), jnp.int32),
             pltpu.VMEM((width, dim), jnp.float32),
             pltpu.VMEM((count, dim), jnp.float32),
             pltpu.VMEM((8, own, dim), jnp.float32),
@@ -553,10 +549,10 @@
             pltpu.SemaphoreType.DMA((copies,)),
         ],
         compiler_params=pltpu.CompilerParams(
-            collective_id=0, has_side_effects=True, vmem_limit_bytes=67043328
+            collective_id=0, has_side_effects=True, vmem_limit_bytes=60 * 2**20
         ),
         name="step",
-    )(queries, documents, jnp.tile(partner[None, :], (8, 2)))
+    )(queries, documents, partner[None, :])
 
 
 def solution(mesh):

time: 67.4 us -> 64.4 us (0.955)
  local copies, waits for them, and re-layouts: 4.06 us -> 1.59 us
    another operation x3 -> x0, local copies, waits for them, and re-layouts: 1.34 us -> none  [on_device(): jnp.tile(partner[None, :], (8, 2))]
    unnamed x4 -> x2, local copies, waits for them, and re-layouts: 2.73 us -> 1.59 us
where the time goes in v7:
time: 64.4 us; the launch traced here: 64.3 us
  Pallas kernels  62.1 us (96%)
  local copies, waits for them, and re-layouts  1.59 us (2%)
    pallas_call x1, Pallas kernels, on_device(): pl.pallas_call(step_kernel, out_shape=(piece, piece), in_specs=[pl.BlockS...  62.1 us
    unnamed x2, local copies, waits for them, and re-layouts  1.59 us

profile of v7, /device:TPU:1, one launch (start us, length us, event | category | flops | bytes accessed | tf_op | source)
XLA Modules:
  0.0 64.3 jit_solution(8680338379359721310)
XLA Ops:
  0.6 62.1 %step.1 = (f32[64,2048]{1,0:T(8,128)S(1)}, f32[64,2048]{1,0:T(8,128)S(1)}) custom-call(bf16[64,2048]{1,0:T(8,128)(2,1)} %q_ref.1, bf16[64,2048]{1,0:T(8,128)(2,1)} %d_ref.1, s32[1,64]{1,0:T(1,128)} %bitcast.1), custom_call_target="tpu_custom_call" | custom-call | tf_op jit(solution)/shard_map/step/pallas_call | solution.py:520
  62.7 0.8 %copy.7 = f32[64,2048]{1,0:T(8,128)} copy(f32[64,2048]{1,0:T(8,128)S(1)} %get-tuple-element.2) | data formatting | bytes 1048576
  63.5 0.8 %copy.8 = f32[64,2048]{1,0:T(8,128)} copy(f32[64,2048]{1,0:T(8,128)S(1)} %get-tuple-element.3) | data formatting | bytes 1048576

commit v8 on v7

--- a/solution.py
+++ b/solution.py
@@ -341,6 +341,9 @@
 
         lax.fori_loop(0, count // own, band_block, 0)
 
+    edge = split_at(dim)
+    early, late = slice(0, edge), slice(edge, dim)
+
     def bounds(nested):
         return slice(0, narrow) if nested < few else slice(lowers[nested], uppers[nested])
 
@@ -373,9 +376,10 @@
             pd_ref,
             at,
         )
-        for pair in (1, 0):
-            theirs = pd_ref.at[d_rows(step, pair, 1), :]
-            across[step, pair] = send(theirs, sib.at[step * 2 + pair], sibling)
+        for pair, cols in ((1, late), (1, early), (0, early), (0, late)):
+            across[step, pair, cols.start] = send(
+                pd_ref.at[d_rows(step, pair, 1), cols], sib.at[step * 2 + pair, :, cols], sibling
+            )
 
     def queries_at(chip):
         piece = 2 * own
@@ -396,7 +400,7 @@
         return pq_ref[pl.ds(pl.multiple_of(start, half), size), cols]
 
     def d_part(step, pair, lo, size, cols):
-        arrive(across[step, pair])
+        arrive(across[step, pair, cols.start])
         mine = pd_ref[d_rows(step, pair, 0, lo, size), cols]
         return mine + sib[step * 2 + pair, pl.ds(lo, size), cols]
 
@@ -408,8 +412,6 @@
             waited.append(copy)
 
     lanes = ((q_part, *neighbours("y")), (d_part, *neighbours("x")))
-    edge = split_at(dim)
-    early, late = slice(0, edge), slice(edge, dim)
     crossed, far, near = {}, {}, {}
 
     def cross(which, step):
@@ -475,25 +477,26 @@
     cross(0, 2)
     send_far(0, 1, early)
     send_far(0, 0, early)
-    queries_at(3 - odd)
+    cross(0, 0)
+    documents_for(1)
     cross(1, 2)
     send_far(1, 1, early)
     send_far(1, 0, early)
-    for step in (1, 3, 0):
-        cross(0, step)
-    documents_for(1)
     documents_for(3)
-    for which in range(2):
-        send_far(which, 0, late)
     cross(1, 1)
+    queries_at(3 - odd)
     cross(1, 3)
-    for which in range(2):
-        send_near(which, 1, early)
+    cross(0, 1)
+    cross(0, 3)
+    send_near(0, 1, early)
+    send_far(0, 0, late)
+    send_near(1, 1, early)
+    send_far(1, 0, late)
     documents_for(0)
-    for which in range(2):
+    cross(1, 0)
+    for which in (0, 1):
         send_near(which, 0, early)
-    cross(1, 0)
-    for which in range(2):
+    for which in (0, 1):
         send_near(which, 0, late)
     outs = (gq_ref, gd_ref)
     last = []

time: 64.4 us -> 63.1 us (0.980)
  Pallas kernels: 62.1 us -> 60.8 us
    pallas_call x1, Pallas kernels: 62.1 us -> 60.8 us  [on_device(): pl.pallas_call(step_kernel, out_shape=(piece, piece), in_specs=[pl.BlockS...]
where the time goes in v8:
time: 63.1 us; the launch traced here: 63 us
  Pallas kernels  60.8 us (96%)
  local copies, waits for them, and re-layouts  1.59 us (3%)
  between operations  0.64 us (1%)
    pallas_call x1, Pallas kernels, on_device(): pl.pallas_call(step_kernel, out_shape=(piece, piece), in_specs=[pl.BlockS...  60.8 us
    unnamed x2, local copies, waits for them, and re-layouts  1.59 us

profile of v8, /device:TPU:1, one launch (start us, length us, event | category | flops | bytes accessed | tf_op | source)
XLA Modules:
  0.0 63.0 jit_solution(13148535204550845871)
XLA Ops:
  0.6 60.8 %step.1 = (f32[64,2048]{1,0:T(8,128)S(1)}, f32[64,2048]{1,0:T(8,128)S(1)}) custom-call(bf16[64,2048]{1,0:T(8,128)(2,1)} %q_ref.1, bf16[64,2048]{1,0:T(8,128)(2,1)} %d_ref.1, s32[1,64]{1,0:T(1,128)} %bitcast.1), custom_call_target="tpu_custom_call" | custom-call | tf_op jit(solution)/shard_map/step/pallas_call | solution.py:523
  61.4 0.8 %copy.7 = f32[64,2048]{1,0:T(8,128)} copy(f32[64,2048]{1,0:T(8,128)S(1)} %get-tuple-element.2) | data formatting | bytes 1048576
  62.2 0.8 %copy.8 = f32[64,2048]{1,0:T(8,128)} copy(f32[64,2048]{1,0:T(8,128)S(1)} %get-tuple-element.3) | data formatting | bytes 1048576

commit v9 on v8

--- a/solution.py
+++ b/solution.py
@@ -235,17 +235,18 @@
     taken = [
         pltpu.make_async_copy(d_ref, docs_ref.at[d_place, :], inside.at[0]),
         pltpu.make_async_copy(q_ref, rows_ref.at[q_place, :], inside.at[1]),
+        pltpu.make_async_copy(p_ref, marks.at[place_of_row(0, 0)], inside.at[2]),
     ]
     for copy in taken:
         copy.start()
     meet([*neighbours("y"), *neighbours("x"), sibling])
     for copy in taken:
         copy.wait()
-    marks[place_of_row(0, 0)] = p_ref[...]
     lse[...] = jnp.zeros_like(lse)
     peaks[...] = jnp.zeros_like(peaks)
     gather(send, rows_ref, docs_ref, own)
-    marked = [send(p_ref, marks.at[place_of_row(0, 0)], device) for _, _, device in row_peers()]
+    mark = marks.at[place_of_row(0, 0)]
+    marked = [send(mark, mark, device) for _, _, device in row_peers()]
 
     turn = width // 2
     tall = count // 2
@@ -523,7 +524,7 @@
     return pl.pallas_call(
         step_kernel,
         out_shape=(piece, piece),
-        in_specs=[pl.BlockSpec(memory_space=pl.ANY)] * 2 + [VMEM],
+        in_specs=[pl.BlockSpec(memory_space=pl.ANY)] * 3,
         out_specs=(VMEM, VMEM),
         scratch_shapes=[
             pltpu.VMEM((width, dim), wire),
@@ -547,7 +548,7 @@
             pltpu.VMEM((2, own, edge), wire),
             pltpu.VMEM((2, 4, own, dim - edge), wire),
             pltpu.VMEM((2, 4, own, dim - edge), wire),
-            pltpu.SemaphoreType.DMA((2,)),
+            pltpu.SemaphoreType.DMA((3,)),
             pltpu.SemaphoreType.DMA((copies,)),
             pltpu.SemaphoreType.DMA((copies,)),
         ],

time: 63.1 us -> 62.6 us (level)
  no operation moved by 1% of the time
where the time goes in v9:
time: 62.6 us; the launch traced here: 62.5 us
  Pallas kernels  60.2 us (96%)
  local copies, waits for them, and re-layouts  1.59 us (3%)
  between operations  0.64 us (1%)
    pallas_call x1, Pallas kernels, on_device(): pl.pallas_call(step_kernel, out_shape=(piece, piece), in_specs=[pl.BlockS...  60.2 us
    unnamed x2, local copies, waits for them, and re-layouts  1.59 us

profile of v9, /device:TPU:1, one launch (start us, length us, event | category | flops | bytes accessed | tf_op | source)
XLA Modules:
  0.0 62.5 jit_solution(18085864806170312693)
XLA Ops:
  0.6 60.2 %step.1 = (f32[64,2048]{1,0:T(8,128)S(1)}, f32[64,2048]{1,0:T(8,128)S(1)}) custom-call(bf16[64,2048]{1,0:T(8,128)(2,1)} %q_ref.1, bf16[64,2048]{1,0:T(8,128)(2,1)} %d_ref.1, s32[1,64]{1,0:T(1,128)} %bitcast.1), custom_call_target="tpu_custom_call" | custom-call | tf_op jit(solution)/shard_map/step/pallas_call | solution.py:524
  60.9 0.8 %copy.7 = f32[64,2048]{1,0:T(8,128)} copy(f32[64,2048]{1,0:T(8,128)S(1)} %get-tuple-element.2) | data formatting | bytes 1048576
  61.7 0.8 %copy.8 = f32[64,2048]{1,0:T(8,128)} copy(f32[64,2048]{1,0:T(8,128)S(1)} %get-tuple-element.3) | data formatting | bytes 1048576

commit v10 on v9

--- a/solution.py
+++ b/solution.py
@@ -483,13 +483,13 @@
     cross(1, 2)
     send_far(1, 1, early)
     send_far(1, 0, early)
-    documents_for(3)
+    queries_at(3 - odd)
     cross(1, 1)
-    queries_at(3 - odd)
-    cross(1, 3)
     cross(0, 1)
     cross(0, 3)
+    documents_for(3)
     send_near(0, 1, early)
+    cross(1, 3)
     send_far(0, 0, late)
     send_near(1, 1, early)
     send_far(1, 0, late)

time: 62.6 us -> 62.6 us (level)
  no operation moved by 1% of the time
where the time goes in v10:
time: 62.6 us; the launch traced here: 62.5 us
  Pallas kernels  60.2 us (96%)
  local copies, waits for them, and re-layouts  1.59 us (3%)
  between operations  0.64 us (1%)
    pallas_call x1, Pallas kernels, on_device(): pl.pallas_call(step_kernel, out_shape=(piece, piece), in_specs=[pl.BlockS...  60.2 us
    unnamed x2, local copies, waits for them, and re-layouts  1.59 us

profile of v10, /device:TPU:1, one launch (start us, length us, event | category | flops | bytes accessed | tf_op | source)
XLA Modules:
  0.0 62.5 jit_solution(10620522020125445602)
XLA Ops:
  0.6 60.2 %step.1 = (f32[64,2048]{1,0:T(8,128)S(1)}, f32[64,2048]{1,0:T(8,128)S(1)}) custom-call(bf16[64,2048]{1,0:T(8,128)(2,1)} %q_ref.1, bf16[64,2048]{1,0:T(8,128)(2,1)} %d_ref.1, s32[1,64]{1,0:T(1,128)} %bitcast.1), custom_call_target="tpu_custom_call" | custom-call | tf_op jit(solution)/shard_map/step/pallas_call | solution.py:524
  60.9 0.8 %copy.7 = f32[64,2048]{1,0:T(8,128)} copy(f32[64,2048]{1,0:T(8,128)S(1)} %get-tuple-element.2) | data formatting | bytes 1048576
  61.7 0.8 %copy.8 = f32[64,2048]{1,0:T(8,128)} copy(f32[64,2048]{1,0:T(8,128)S(1)} %get-tuple-element.3) | data formatting | bytes 1048576
